TPU v7x, 256 devices: a whole 4x4x8 slice. The times are simulated.
256 devices in a mesh: expert: 8 (over z), tensor: 4 (over y), dp: 8 (over x, core).
Axes of the slice: x: 4, y: 4, z: 8, core: 2. Of those that a mesh axis runs over, the one named last changes fastest.
Arguments:
- hidden_in: bfloat16 [8, 512, 4096], P('dp', 'expert'), may hold values from -64 to 64
- expert_ids: int32 [8, 512, 2], P('dp', 'expert'), may hold values from 0 to 7, all different within a row; in each aligned block of 64 rows (0 to 63, 64 to 127, ..., all dimensions but the last counted through in order) at most 18 rows name the same one
- ffn_gain: float32 [4096], replicated, may hold values from 0.5 to 1.5
- w_router: bfloat16 [4096, 8], replicated, may hold values from -0.09375 to 0.09375
- w_gate: bfloat16 [8, 4096, 14336], P('expert', None, ('tensor', 'dp')), may hold values from -0.09375 to 0.09375
- w_up: bfloat16 [8, 4096, 14336], P('expert', None, ('tensor', 'dp')), may hold values from -0.09375 to 0.09375
- w_down: bfloat16 [8, 14336, 4096], P('expert', ('tensor', 'dp')), may hold values from -0.046875 to 0.046875
Outputs:
- hidden_out: bfloat16 [8, 512, 4096], P('dp', 'expert', 'tensor')
- layer_score: float32 [], replicated
Inputs may be any that keep to these rules, and one draw needn't show every extreme that they name: `expert_ids`: among the 64 tokens of one device (aligned blocks of the flattened sequence and position order), no expert is chosen by more than 18 of them; a token's two experts differ.
All inputs are finite; a program needn't handle non-finite values.
Results may differ from a plain program's by a relative error of at most 0.0027.
Values may be sent and summed in bfloat16 or wider, within the bound.
A program may use at most 128 MiB of HBM per device.

v0:
```python
import jax
import jax.numpy as jnp
from jax import lax
from jax.sharding import PartitionSpec as P

EPS_NORM = 1e-05
EPS_COS = 1e-06


def from_everyone(shard, axis):
    copies = jnp.broadcast_to(shard, (lax.axis_size(axis), *shard.shape))
    return lax.all_to_all(copies, axis, split_axis=0, concat_axis=0, tiled=True)


def of_everyone(shard, axis):
    return from_everyone(shard, axis).sum(axis=0)


def packed_total(arrays, axis):
    ends = [0]
    for a in arrays:
        ends.append(ends[-1] + a.size)
    total = of_everyone(jnp.concatenate([a.ravel() for a in arrays]), axis)
    return tuple((total[b:e].reshape(a.shape) for a, b, e in zip(arrays, ends, ends[1:])))


def slot_positions(flat_ids, experts):
    pair_count = flat_ids.shape[0]
    onehot = (flat_ids[:, None] == jnp.arange(experts, dtype=jnp.int32)[None, :]).astype(jnp.int32)
    positions = jnp.arange(pair_count, dtype=jnp.int32)
    earlier = (positions[None, :] < positions[:, None]).astype(jnp.int32)
    before = jnp.sum(earlier[:, :, None] * onehot[None, :, :], axis=1)
    return jnp.sum(before * onehot, axis=1)


def shards(hidden_in, expert_ids, ffn_gain, w_router, w_gate, w_up, w_down):
    tok_count = hidden_in.shape[1]
    model_width = hidden_in.shape[2]
    top_count = expert_ids.shape[2]
    local_experts = w_gate.shape[0]
    expert_count = lax.axis_size("expert")
    tensor_count = lax.axis_size("tensor")
    replica_count = lax.axis_size("dp")
    experts = expert_count * local_experts
    capacity = max(2, 9 * tok_count * top_count // (8 * experts))
    feature_share = model_width // tensor_count
    token_rows = hidden_in.reshape(tok_count, model_width).astype(jnp.float32)
    in_squares = jnp.mean(token_rows * token_rows, axis=1)
    inverse_rms = lax.rsqrt(in_squares[:, None] + EPS_NORM)
    normed = (token_rows * inverse_rms * ffn_gain[None, :]).astype(jnp.bfloat16)
    logits = jnp.dot(normed, w_router, preferred_element_type=jnp.float32)
    chosen = expert_ids.reshape(tok_count, top_count)
    selector = (chosen[:, :, None] == jnp.arange(experts, dtype=jnp.int32)[None, None, :]).astype(
        jnp.float32
    )
    picked = jnp.sum(selector * logits[:, None, :], axis=2)
    spread = picked[:, 0] - picked[:, 1]
    gate_values = jnp.stack([jax.nn.sigmoid(spread), jax.nn.sigmoid(-spread)], axis=1)
    slot_index = slot_positions(chosen.reshape(-1), experts).reshape(tok_count, top_count)
    destination = chosen * capacity + slot_index
    row_index = jnp.arange(experts * capacity, dtype=jnp.int32)
    matches = destination[None, :, :] == row_index[:, None, None]
    dispatch_matrix = jnp.any(matches, axis=2).astype(jnp.bfloat16)
    outgoing = jnp.dot(dispatch_matrix, normed, preferred_element_type=jnp.float32).astype(
        jnp.bfloat16
    )
    outgoing = outgoing.reshape(expert_count, local_experts, capacity, model_width)
    arrived = lax.all_to_all(outgoing, "expert", split_axis=0, concat_axis=0, tiled=True)
    arrived = arrived[None]
    pieces = lax.all_gather(arrived, "dp", axis=0, tiled=True)
    gate_term = jnp.einsum("snlcd,ldf->snlcf", pieces, w_gate, preferred_element_type=jnp.float32)
    up_term = jnp.einsum("snlcd,ldf->snlcf", pieces, w_up, preferred_element_type=jnp.float32)
    activated = (jax.nn.silu(gate_term) * up_term).astype(jnp.bfloat16)
    hidden_share = w_down.shape[1]
    down_blocks = w_down.reshape(local_experts, hidden_share, tensor_count, feature_share)
    terms = jnp.einsum(
        "snlcf,lftq->tsnlcq", activated, down_blocks, preferred_element_type=jnp.float32
    )
    summed = lax.psum_scatter(
        terms.reshape(
            tensor_count * replica_count, expert_count, local_experts, capacity, feature_share
        ),
        ("tensor", "dp"),
        scatter_dimension=0,
        tiled=True,
    )
    returned = lax.all_to_all(
        summed[0].astype(jnp.bfloat16), "expert", split_axis=0, concat_axis=0, tiled=True
    )
    results = returned.reshape(experts * capacity, feature_share).astype(jnp.float32)
    placed = (destination[:, :, None] == row_index[None, None, :]).astype(jnp.float32)
    weights = jnp.sum(gate_values[:, :, None] * placed, axis=1)
    mixture = jnp.dot(weights, results, precision=lax.Precision.HIGHEST)
    share_start = lax.axis_index("tensor") * feature_share
    own_rows = lax.dynamic_slice_in_dim(token_rows, share_start, feature_share, 1)
    outputs = (own_rows + mixture).astype(jnp.bfloat16)
    out_rows = outputs.astype(jnp.float32)
    cross_sum, out_sum = packed_total(
        (jnp.sum(own_rows * out_rows, axis=1), jnp.sum(out_rows * out_rows, axis=1)), "tensor"
    )
    cosine = (
        cross_sum
        / model_width
        * lax.rsqrt((in_squares + EPS_COS) * (out_sum / model_width + EPS_COS))
    )
    local_total = jnp.sum(1.0 - cosine)
    grand_total = of_everyone(local_total, ("expert", "dp"))
    layer_score = grand_total / (tok_count * expert_count * replica_count)
    return (outputs.reshape(1, tok_count, feature_share), layer_score)


def solution(mesh):
    return jax.shard_map(
        shards,
        mesh=mesh,
        in_specs=(
            P("dp", "expert", None),
            P("dp", "expert", None),
            P(),
            P(),
            P("expert", None, ("tensor", "dp")),
            P("expert", None, ("tensor", "dp")),
            P("expert", ("tensor", "dp"), None),
        ),
        out_specs=(P("dp", "expert", "tensor"), P()),
        check_vma=False,
    )
```

profile of v0, /device:TPU:1, one launch (start us, length us, event | category | flops | bytes accessed | tf_op | source)
XLA Modules:
  0.0 366.2 jit_solution(16939291626299301986)
XLA Ops:
  7.2 0.8 copy.75
  8.3 2.3 multiply_reduce_fusion
  11.0 0.7 add_bitcast_fusion
  11.7 1.2 fusion.13
  13.0 1.6 convolution_convert_fusion
  15.0 47.4 %all_to_all.22 = bf16[8,1,18,4096]{3,2,1,0:T(8,128)(2,1)S(1)} all-to-all(bf16[8,1,18,4096]{3,2,1,0:T(8,128)(2,1)S(1)} %bitcast.88), channel_id=1, replica_groups=mesh['expert'=8,'tensor'=4,'dp'=8] {'expert'}, dimensions={0} | all-to-all | bytes 2359296 | tf_op jit(solution)/shard_map/all_to_all | solution.py:68
  62.4 1.7 copy.81
  64.2 7.2 %reshape.132 = bf16[448,4,1024]{2,1,0:T(4,128)(2,1)} reshape(bf16[1,448,4096]{2,1,0:T(8,128)(2,1)} %param.13) | data formatting | bytes 7340032 | tf_op jit(solution)/shard_map/reshape.6
  71.4 47.9 %all-gather.3.cloned.1.call-done = bf16[64,1,18,4096]{3,0,2,1:T(8,128)(2,1)} async-done(((bf16[8,1,18,4096]{3,0,2,1:T(8,128)(2,1)}), bf16[64,1,18,4096]{3,0,2,1:T(8,128)(2,1)}) %all-gather.3.cloned.1.call-update) | async-done | bytes 9437200 | tf_op jit(solution)/shard_map/all_gather | solution.py:70
  119.3 8.7 %copy.82 = bf16[64,1,18,4096]{3,2,0,1:T(8,128)(2,1)S(1)} copy(bf16[64,1,18,4096]{3,0,2,1:T(8,128)(2,1)} %all-gather.3.cloned.1.call-done) | data formatting | bytes 18874368 | tf_op jit(solution)/shard_map/all_gather | solution.py:70
  128.0 8.8 %fusion = f32[8,8,18,448]{3,2,1,0:T(8,128)} fusion(bf16[8,8,18,4096]{3,2,1,0:T(8,128)(2,1)S(1)} %bitcast.86, bf16[1,4096,448]{1,2,0:T(8,128)(2,1)S(1)} %copy-done.5), kind=kOutput, calls=%fused_computation.2 | convolution fusion | flops 4227858432 | bytes 15171584 | tf_op jit(solution)/shard_map/snlcd,ldf->snlcf/dot_general | solution.py:72
  136.8 10.2 %fusion.5 = bf16[8,8,1,18,448]{4,3,1,0,2:T(8,128)(2,1)S(1)} fusion(f32[8,8,18,448]{3,2,1,0:T(8,128)} %fusion, bf16[8,8,18,4096]{3,2,1,0:T(8,128)(2,1)S(1)} %bitcast.87, bf16[1,4096,448]{1,2,0:T(8,128)(2,1)S(1)} %copy-done.6), kind=kOutput, calls=%fused_computation.8 | convolution fusion | flops 4230955008 | bytes 16203776 | tf_op jit(solution)/shard_map/snlcd,ldf->snlcf/dot_general | solution.py:71
  146.9 12.1 %convolution_bitcast_fusion = f32[4,8,8,1,18,1024]{5,4,0,2,1,3:T(8,128)} fusion(bf16[448,4,1024,1,1]{2,1,0,4,3:T(4,128)(2,1)S(1)} %bitcast.89, bf16[8,8,1,18,448]{4,3,1,0,2:T(8,128)(2,1)S(1)} %fusion.5), kind=kOutput, calls=%fused_computation | convolution fusion | flops 4227858432 | bytes 23576576 | tf_op jit(solution)/shard_map/snlcf,lftq->tsnlcq/dot_general | solution.py:76
  159.1 21.7 %copy.84 = f32[4,8,8,1,18,1024]{5,2,4,3,1,0:T(8,128)} copy(f32[4,8,8,1,18,1024]{5,4,0,2,1,3:T(8,128)} %convolution_bitcast_fusion) | data formatting | bytes 37748736 | tf_op jit(solution)/shard_map/snlcf,lftq->tsnlcq/transpose | solution.py:76
  180.8 1.0 copy-done.1
  182.1 126.4 %reduce-scatter.2.cloned.1.call-done = f32[1,8,1,18,1024]{4,1,3,2,0:T(8,128)} async-done(((f32[32,8,1,18,1024]{4,1,3,2,0:T(8,128)}), f32[1,8,1,18,1024]{4,1,3,2,0:T(8,128)}) %reduce-scatter.2.cloned.1.call-update) | async-done | bytes 589840 | tf_op jit(solution)/shard_map/reduce_scatter | solution.py:79
  308.6 1.1 convert_bitcast_fusion
  309.7 0.9 copy.85
  310.6 6.8 %all-to-all-start.1 = ((bf16[8,1,18,1024]{3,2,1,0:T(8,128)(2,1)}), bf16[8,1,18,1024]{3,2,1,0:T(8,128)(2,1)S(1)}, u32[]{:S(2)}, u32[]{:S(2)}) async-start(bf16[8,1,18,1024]{3,2,1,0:T(8,128)(2,1)} %copy.85), calls=%async_computation.2 | async-start | bytes 786432 | tf_op jit(solution)/shard_map/all_to_all | solution.py:87
  317.9 11.7 %all-to-all-done.1 = bf16[8,1,18,1024]{3,2,1,0:T(8,128)(2,1)S(1)} async-done(((bf16[8,1,18,1024]{3,2,1,0:T(8,128)(2,1)}), bf16[8,1,18,1024]{3,2,1,0:T(8,128)(2,1)S(1)}, u32[]{:S(2)}, u32[]{:S(2)}) %all-to-all-start.1) | async-done | bytes 294944 | tf_op jit(solution)/shard_map/all_to_all | solution.py:87
  329.7 1.1 fusion.16
  330.8 6.9 %all_to_all.23 = f32[4,1,128]{2,1,0:T(1,128)S(1)} all-to-all(f32[4,1,128]{2,1,0:T(1,128)S(1)} %broadcast_in_dim.7), channel_id=1, replica_groups=mesh['expert'=8,'tensor'=4,'dp'=8] {'tensor'}, dimensions={0} | all-to-all | bytes 4096 | tf_op jit(solution)/shard_map/all_to_all | solution.py:12
  337.8 0.7 subtract_reduce_fusion
  339.1 17.8 %all_to_all.24 = f32[64,1,1]{2,1,0:T(1,128)S(1)} all-to-all(f32[64,1,1]{2,1,0:T(1,128)S(1)} %broadcast_in_dim.8), channel_id=1, replica_groups=mesh['expert'=8,'tensor'=4,'dp'=8] {'expert','dp'}, dimensions={0} | all-to-all | bytes 512 | tf_op jit(solution)/shard_map/all_to_all | solution.py:12
  (42 shorter events, 3.6 us)
Async XLA Ops:
  7.2 173.6 %copy-start = (bf16[4096,8]{0,1:T(8,128)(2,1)S(1)}, bf16[4096,8]{0,1:T(8,128)(2,1)}, u32[]{:S(2)}) copy-start(bf16[4096,8]{0,1:T(8,128)(2,1)} %param.10) | copy-start | bytes 196612
  7.2 112.1 %all-gather.3.cloned.1.call-start = ((), (), s32[]{:S(2)}) async-start(), calls=%async_computation.6 | async-start | bytes 10616832 | tf_op jit(solution)/shard_map/all_gather | solution.py:70
  64.1 244.4 %reduce-scatter.2.cloned.1.call-start = ((), (), s32[]{:S(2)}) async-start(), calls=%async_computation.5 | async-start | bytes 19464192 | tf_op jit(solution)/shard_map/reduce_scatter | solution.py:79
  119.3 8.7 %copy-start.5 = (bf16[1,4096,448]{1,2,0:T(8,128)(2,1)S(1)}, bf16[1,4096,448]{1,2,0:T(8,128)(2,1)}, u32[]{:S(2)}) copy-start(bf16[1,4096,448]{1,2,0:T(8,128)(2,1)} %param.12) | copy-start | bytes 11010052
  128.0 8.8 %copy-start.6 = (bf16[1,4096,448]{1,2,0:T(8,128)(2,1)S(1)}, bf16[1,4096,448]{1,2,0:T(8,128)(2,1)}, u32[]{:S(2)}) copy-start(bf16[1,4096,448]{1,2,0:T(8,128)(2,1)} %param.11) | copy-start | bytes 11010052
  136.8 10.2 %copy-start.2 = (bf16[448,4,1024]{2,1,0:T(4,128)(2,1)S(1)}, bf16[448,4,1024]{2,1,0:T(4,128)(2,1)}, u32[]{:S(2)}) copy-start(bf16[448,4,1024]{2,1,0:T(4,128)(2,1)} %reshape.132) | copy-start | bytes 11010052
  180.8 1.0 copy-start.1
  180.8 1.0 copy-start.3
  180.8 1.4 copy-start.4
  310.6 19.0 %all-to-all-start.1 = ((bf16[8,1,18,1024]{3,2,1,0:T(8,128)(2,1)}), bf16[8,1,18,1024]{3,2,1,0:T(8,128)(2,1)S(1)}, u32[]{:S(2)}, u32[]{:S(2)}) async-start(bf16[8,1,18,1024]{3,2,1,0:T(8,128)(2,1)} %copy.85), calls=%async_computation.2 | async-start | bytes 786432 | tf_op jit(solution)/shard_map/all_to_all | solution.py:87
Sparse Core Ops, SparseCore 0:
  64.3 54.9 all-gather.2
  180.9 127.6 reduce-scatter.1
where the time goes:
time: 367 us; the launch traced here: 366 us
  waiting for transfers between devices  186 us (51%)
  blocking collectives  72.2 us (20%)
  local copies, waits for them, and re-layouts  43.7 us (12%)
  matrix products  34.1 us (9%)
  between operations  16 us (4%)
  other arithmetic  7.32 us (2%)
  starting transfers between devices  6.92 us (2%)
    reduce_scatter x1, waiting for transfers between devices, shards(): lax.psum_scatter(terms.reshape(tensor_count * replica_count, expert_count...  126 us
    all_gather x1, waiting for transfers between devices, shards(): pieces = lax.all_gather(arrived, 'dp', axis=0, tiled=True)  47.9 us
    all_to_all x1, blocking collectives, shards(): lax.all_to_all(outgoing, 'expert', split_axis=0, concat_axis=0, tiled=True)  47.4 us
    all_to_all x2, blocking collectives, from_everyone(): return lax.all_to_all(copies, axis, split_axis=0, concat_axis=0, tiled=True)  24.8 us
    transpose x1, local copies, waits for them, and re-layouts, shards(): jnp.einsum('snlcf,lftq->tsnlcq', activated, down_blocks, preferred_elemen...  21.7 us
    dot_general x1, matrix products, shards(): jnp.einsum('snlcf,lftq->tsnlcq', activated, down_blocks, preferred_elemen...  12.1 us
    all_to_all x1, waiting for transfers between devices, shards(): lax.all_to_all(summed[0].astype(jnp.bfloat16), 'expert', split_axis=0, co...  11.7 us
    dot_general x1, matrix products, shards(): jnp.einsum('snlcd,ldf->snlcf', pieces, w_gate, preferred_element_type=jnp...  10.2 us
  transfers between devices with their start and end apart: 3, of which 3 were waited for; matrix products, arithmetic and copies ran while one was open for 2% of the time, Pallas kernels for 0%

commit v1 on v0

v1 whole, which is shorter than its diff:
```python
import functools

import jax
import jax.numpy as jnp
from jax import lax
from jax.experimental import pallas as pl
from jax.experimental.pallas import tpu as pltpu
from jax.sharding import PartitionSpec as P

EPS_NORM = 1e-05
EPS_COS = 1e-06
BF = jnp.bfloat16
F32 = jnp.float32
RING = 4
MAIN = 16


class Links:
    def __init__(self, send_sems, recv_sems):
        self.send_sems, self.recv_sems, self.count, self.started = send_sems, recv_sems, 0, []

    def send(self, src, dst, device):
        n = self.count
        self.count += 1
        copy = pltpu.make_async_remote_copy(
            src_ref=src,
            dst_ref=dst,
            send_sem=self.send_sems.at[n],
            recv_sem=self.recv_sems.at[n],
            device_id=device,
            device_id_type=pl.DeviceIdType.MESH,
        )
        copy.start()
        self.started.append(copy)
        return copy

    def drain(self):
        for copy in self.started:
            copy.wait_send()


def mod(value, n):
    return lax.rem(value + 2 * n, n)


def dot(a, b):
    return jnp.dot(a, b, preferred_element_type=F32)


def onehot(mask):
    return jnp.where(mask, 1.0, 0.0).astype(BF)


def kernel(
    sizes,
    h_ref, ids_ref, gain_ref, router_ref, wg_hbm, wu_hbm, wd_hbm,
    out_ref, score_ref,
    wg, wu, wd, normed, keep, sent, got, back_sent, back,
    xa, xb, ga, ua, act, pa, pb, qa, qb, ra, rb, ta, tb, sa, sb, res,
    sums, totals, grand,
    send_sems, recv_sems, weight_sems,
):
    experts, cap = sizes
    tokens, width = h_ref.shape
    share = width // RING
    lanes = share // RING
    rows = experts * cap
    spread_rows = experts * MAIN
    per_lane = MAIN // 2
    z = lax.axis_index("expert")
    t = lax.axis_index("tensor")
    d = lax.axis_index("dp")
    x, c = d // 2, lax.rem(d, 2)
    other = 1 - c
    x_of = lambda pos: {"dp": pos * 2 + c}
    y_of = lambda pos: {"tensor": pos}
    partner = {"dp": x * 2 + other}
    dp_count = RING * 2

    barrier = pltpu.get_barrier_semaphore()
    peers = (
        [{"expert": mod(z + k, experts)} for k in range(1, experts)]
        + [{"tensor": mod(t + k, RING)} for k in range(1, RING)]
        + [{"dp": mod(d + k, dp_count)} for k in range(1, dp_count)]
    )
    for peer in peers:
        pl.semaphore_signal(barrier, inc=1, device_id=peer, device_id_type=pl.DeviceIdType.MESH)

    weights = [
        pltpu.make_async_copy(src, dst, weight_sems.at[n])
        for n, (src, dst) in enumerate(((wg_hbm, wg), (wu_hbm, wu), (wd_hbm, wd)))
    ]
    for copy in weights:
        copy.start()

    token_rows = h_ref[...].astype(F32)
    in_squares = jnp.sum(token_rows * token_rows, axis=1, keepdims=True) / width
    normed[...] = (token_rows * lax.rsqrt(in_squares + EPS_NORM) * gain_ref[...]).astype(BF)
    logits = dot(normed[...], router_ref[...])
    lane = lax.broadcasted_iota(jnp.int32, (tokens, 128), 1)
    lane_f = lane.astype(F32)
    first, second = ids_ref[:, 0:1], ids_ref[:, 1:2]
    first_f, second_f = first.astype(F32), second.astype(F32)
    is_first = jnp.where(lane == first, 1.0, 0.0)
    is_second = jnp.where(lane == second, 1.0, 0.0)
    spread = jnp.sum((is_first[:, :experts] - is_second[:, :experts]) * logits, axis=1, keepdims=True)
    gate_first = 1.0 / (1.0 + jnp.exp(-spread))
    gate_second = 1.0 / (1.0 + jnp.exp(spread))
    earlier = onehot(
        lax.broadcasted_iota(jnp.int32, (tokens, tokens), 1)
        < lax.broadcasted_iota(jnp.int32, (tokens, tokens), 0)
    )
    before = dot(earlier, (is_first + is_second).astype(BF))
    kept = [in_squares, gate_first, gate_second]
    for chosen, mask in ((first_f, is_first), (second_f, is_second)):
        slot = jnp.sum(before * mask, axis=1, keepdims=True)
        place = chosen * MAIN + slot
        kept.append(jnp.where(slot < MAIN, place, -1.0))
        kept.append(jnp.where(slot < MAIN, -1000.0, place - MAIN))
    for n, column in enumerate(kept):
        keep[n] = jnp.broadcast_to(column, (tokens, 128))

    def chosen_masks(n, shift):
        return onehot(lane_f - shift == keep[n])

    main = (chosen_masks(3, 0.0) + chosen_masks(5, 0.0)).astype(F32).T.astype(BF)
    extra = jnp.zeros((spread_rows, 128), F32)
    for k in range(per_lane):
        picks = (chosen_masks(4, 2.0 * k) + chosen_masks(6, 2.0 * k)).astype(F32).T.astype(BF)
        block = normed[:, pl.ds(pl.multiple_of(t * share + k * 128, 128), 128)]
        extra = extra + dot(picks[:spread_rows], block)
    for q in range(RING):
        block = normed[:, pl.ds(pl.multiple_of(t * share + q * lanes, 128), lanes)]
        picked = dot(main[:spread_rows], block).astype(BF)
        sent[:, :, q * lanes : (q + 1) * lanes] = picked.reshape(experts, MAIN, lanes)
    sent[:, :, share:] = extra.astype(BF).reshape(experts, MAIN, 128)

    ga[...] = jnp.zeros_like(ga)
    ua[...] = jnp.zeros_like(ua)
    pl.semaphore_wait(barrier, len(peers))
    links = Links(send_sems, recv_sems)

    def exchange(src, dst):
        copies = []
        for k in sorted(range(1, experts), key=lambda k: -min(k, experts - k)):
            to = mod(z + k, experts)
            copies.append(links.send(src.at[to], dst.at[z], {"expert": to}))
        dst[z] = src[z]
        for copy in copies:
            copy.wait_recv()

    exchange(sent, got)

    def placing(transposed):
        shape = (spread_rows, rows) if transposed else (rows, spread_rows)
        row = lax.broadcasted_iota(jnp.int32, shape, 1 if transposed else 0)
        place = lax.broadcasted_iota(jnp.int32, shape, 0 if transposed else 1)
        source, slot = place // MAIN, place % MAIN
        base = source * cap
        fits = (MAIN + slot % 2) < cap
        extras = [
            onehot((row == base + MAIN + slot % 2) & (slot // 2 == k) & fits) for k in range(per_lane)
        ]
        return onehot((row == base + slot) & (slot < cap)), extras

    put, put_extra = placing(False)
    extras = got[:, :, share:].reshape(spread_rows, 128)
    for q in range(RING):
        block = dot(put, got[:, :, q * lanes : (q + 1) * lanes].reshape(spread_rows, lanes))
        halves = [dot(put_extra[k], extras) for k in range(q * lanes // 128, (q + 1) * lanes // 128)]
        block = (block + jnp.concatenate(halves, axis=1)).astype(BF)
        if q < 2:
            xa[x, q, t, c] = block
        else:
            xb[t, q - 2, x, c] = block

    class Gather:
        def __init__(self, view, me, device_of):
            self.view = view
            self.left, self.right = mod(me - 1, RING), mod(me + 1, RING)
            self.to_left, self.to_right = device_of(self.left), device_of(self.right)
            send = lambda pos, q, to: links.send(view(pos, q), view(pos, q), to)
            self.from_left = [send(me, 0, self.to_right)]
            self.from_right = [send(me, 1, self.to_left)]
            self.from_left.append(send(me, 1, self.to_right))
            self.from_right.append(send(me, 0, self.to_left))

        def pass_on(self):
            self.from_left[0].wait_recv()
            left = self.view(self.left, 0)
            self.from_left.append(links.send(left, left, self.to_right))
            self.from_right[0].wait_recv()
            right = self.view(self.right, 1)
            self.from_right.append(links.send(right, right, self.to_left))

        def wait_left(self):
            self.from_left[1].wait_recv()

        def wait_right(self):
            self.from_right[1].wait_recv()

        def wait_far(self):
            self.from_left[2].wait_recv()
            self.from_right[2].wait_recv()

    small_a = Gather(lambda pos, q: xa.at[x, q, pos, c], t, y_of)
    small_b = Gather(lambda pos, q: xb.at[t, q, pos, c], x, x_of)
    small_a.pass_on()
    small_b.pass_on()
    for small in (small_a, small_b):
        small.wait_left()
        small.wait_right()
        small.wait_far()
    big_a = Gather(lambda pos, q: xa.at[pos, q, :, c], x, x_of)
    big_b = Gather(lambda pos, q: xb.at[pos, q, :, c], t, y_of)

    def share_core(buf, pos):
        return links.send(buf.at[pos, :, :, c], buf.at[pos, :, :, c], partner)

    m = 2 * rows

    def up_unit_a(pos):
        @pl.loop(0, RING)
        def _(y):
            for w, acc in ((wg, ga), (wu, ua)):
                terms = [dot(xa[pos, q, y].reshape(m, lanes), w[y * RING + q]) for q in range(2)]
                acc[pos] += terms[0] + terms[1]

    def up_unit_b(pos):
        @pl.loop(0, RING)
        def _(xp):
            for w, acc in ((wg, ga), (wu, ua)):
                terms = [dot(xb[pos, q, xp].reshape(m, lanes), w[pos * RING + 2 + q]) for q in range(2)]
                acc[xp] += terms[0] + terms[1]

    own_a, own_b = share_core(xa, x), share_core(xb, t)
    weights[0].wait()
    weights[1].wait()
    own_a.wait_recv()
    up_unit_a(x)
    own_b.wait_recv()
    up_unit_b(t)
    big_a.pass_on()
    big_b.pass_on()
    shared = []
    for big, buf, unit in ((big_a, xa, up_unit_a), (big_b, xb, up_unit_b)):
        big.wait_left()
        shared.append((share_core(buf, big.left), unit, big.left))
        big.wait_right()
        shared.append((share_core(buf, big.right), unit, big.right))
    for copy, unit, pos in shared:
        copy.wait_recv()
        unit(pos)
    far_x, far_y = mod(x + 2, RING), mod(t + 2, RING)
    big_a.wait_far()
    far_a = share_core(xa, far_x)
    big_b.wait_far()
    far_b = share_core(xb, far_y)
    far_a.wait_recv()
    up_unit_a(far_x)
    far_b.wait_recv()
    up_unit_b(far_y)

    weights[2].wait()

    @pl.loop(0, RING)
    def _(xp):
        gate = ga[xp]
        act[xp] = (gate / (1.0 + jnp.exp(-gate)) * ua[xp]).astype(BF)

    def down_unit_a(pos):
        @pl.loop(0, RING)
        def _(y):
            for q in range(2):
                w = wd[:, pl.ds(pl.multiple_of(y * share + q * lanes, 128), lanes)]
                pa[pos, q, y] = dot(act[pos], w).astype(BF).reshape(2, rows, lanes)

        return links.send(pa.at[pos, :, :, other], qa.at[pos], partner)

    def down_unit_b(pos):
        @pl.loop(0, RING)
        def _(xp):
            for q in range(2):
                w = wd[:, pl.ds(pl.multiple_of(pos * share + (2 + q) * lanes, 128), lanes)]
                pb[pos, q, xp] = dot(act[xp], w).astype(BF).reshape(2, rows, lanes)

        return links.send(pb.at[pos, :, :, other], qb.at[pos], partner)

    def add_pair(copy, part, came, pos):
        copy.wait_recv()

        @pl.loop(0, RING)
        def _(n):
            for q in range(2):
                part[pos, q, n, c] = (part[pos, q, n, c].astype(F32) + came[pos, q, n].astype(F32)).astype(BF)

    class Scatter:
        def __init__(self, view, slots, me, device_of):
            self.view, self.slots, self.me = view, slots, me
            self.left, self.right, self.far = mod(me - 1, RING), mod(me + 1, RING), mod(me + 2, RING)
            self.to_left, self.to_right = device_of(self.left), device_of(self.right)

        def send_far(self):
            self.rightward = [links.send(self.view(self.far, 0), self.slots.at[0], self.to_right)]
            self.leftward = [links.send(self.view(self.far, 1), self.slots.at[1], self.to_left)]

        def send_right(self):
            self.rightward.append(links.send(self.view(self.right, 1), self.slots.at[2], self.to_right))

        def send_left(self):
            self.leftward.append(links.send(self.view(self.left, 0), self.slots.at[3], self.to_left))

        def send_sums(self, add):
            self.rightward[0].wait_recv()
            add(self.right, 0, self.slots.at[0])
            self.rightward.append(links.send(self.view(self.right, 0), self.slots.at[4], self.to_right))
            self.leftward[0].wait_recv()
            add(self.left, 1, self.slots.at[1])
            self.leftward.append(links.send(self.view(self.left, 1), self.slots.at[5], self.to_left))

        def wait(self):
            for copy in self.rightward[1:] + self.leftward[1:]:
                copy.wait_recv()

        def parts(self, q):
            return (self.slots.at[4], self.slots.at[3]) if q == 0 else (self.slots.at[2], self.slots.at[5])

    rs_a = Scatter(lambda pos, q: pa.at[pos, q, :, c], ra, x, x_of)
    rs_b = Scatter(lambda pos, q: pb.at[pos, q, :, c], rb, t, y_of)

    def adder(part):
        def add(pos, q, slot):
            @pl.loop(0, RING)
            def _(n):
                part[pos, q, n, c] = (part[pos, q, n, c].astype(F32) + slot[n].astype(F32)).astype(BF)

        return add

    pair_a, pair_b = down_unit_a(far_x), down_unit_b(far_y)
    add_pair(pair_a, pa, qa, far_x)
    rs_a.send_far()
    pair_a = down_unit_a(rs_a.right)
    add_pair(pair_b, pb, qb, far_y)
    rs_b.send_far()
    pair_b = down_unit_b(rs_b.right)
    add_pair(pair_a, pa, qa, rs_a.right)
    rs_a.send_right()
    pair_a = down_unit_a(rs_a.left)
    add_pair(pair_b, pb, qb, rs_b.right)
    rs_b.send_right()
    pair_b = down_unit_b(rs_b.left)
    add_pair(pair_a, pa, qa, rs_a.left)
    rs_a.send_left()
    pair_a = down_unit_a(x)
    add_pair(pair_b, pb, qb, rs_b.left)
    rs_b.send_left()
    pair_b = down_unit_b(t)
    rs_a.send_sums(adder(pa))
    rs_b.send_sums(adder(pb))
    add_pair(pair_a, pa, qa, x)
    add_pair(pair_b, pb, qb, t)

    def finish_big(scatter, part, total, me):
        scatter.wait()

        @pl.loop(0, RING)
        def _(n):
            for q in range(2):
                one, two = scatter.parts(q)
                value = part[me, q, n, c].astype(F32) + one[n].astype(F32) + two[n].astype(F32)
                total[n, q] = value.astype(BF)

    finish_big(rs_a, pa, ta, x)
    last_a = Scatter(lambda pos, q: ta.at[pos, q], sa, t, y_of)
    last_a.send_far()
    last_a.send_right()
    last_a.send_left()
    finish_big(rs_b, pb, tb, t)
    last_b = Scatter(lambda pos, q: tb.at[pos, q], sb, x, x_of)
    last_b.send_far()
    last_b.send_right()
    last_b.send_left()

    def small_adder(total):
        def add(pos, q, slot):
            total[pos, q] = (total[pos, q].astype(F32) + slot[...].astype(F32)).astype(BF)

        return add

    last_a.send_sums(small_adder(ta))
    last_b.send_sums(small_adder(tb))
    for first_q, scatter, total in ((0, last_a, ta), (2, last_b, tb)):
        scatter.wait()
        for q in range(2):
            one, two = scatter.parts(q)
            value = total[scatter.me, q].astype(F32) + one[...].astype(F32) + two[...].astype(F32)
            res[first_q + q] = value.astype(BF)

    take, take_extra = placing(True)
    extra = jnp.zeros((spread_rows, 128), F32)
    for q in range(RING):
        block = res[q]
        back_sent[:, :, q * lanes : (q + 1) * lanes] = dot(take, block).astype(BF).reshape(experts, MAIN, lanes)
        for k in range(lanes // 128):
            extra = extra + dot(take_extra[q * lanes // 128 + k], block[:, k * 128 : (k + 1) * 128])
    back_sent[:, :, share:] = extra.astype(BF).reshape(experts, MAIN, 128)
    exchange(back_sent, back)

    extras = back[:, :, share:].reshape(spread_rows, 128)
    cross = jnp.zeros((tokens, 1), F32)
    squares = jnp.zeros((tokens, 1), F32)
    for k in range(share // 128):
        block = back[:, :, k * 128 : (k + 1) * 128].reshape(spread_rows, 128)
        mixture = jnp.zeros((tokens, 128), F32)
        for gate, n in ((1, 3), (2, 5)):
            picked = dot(chosen_masks(n, 0.0)[:, :spread_rows], block)
            picked = picked + dot(chosen_masks(n + 1, 2.0 * k)[:, :spread_rows], extras)
            mixture = mixture + keep[gate] * picked
        own = h_ref[:, pl.ds(pl.multiple_of(t * share + k * 128, 128), 128)].astype(F32)
        output = (own + mixture).astype(BF)
        out_ref[:, k * 128 : (k + 1) * 128] = output
        output = output.astype(F32)
        cross = cross + jnp.sum(own * output, axis=1, keepdims=True)
        squares = squares + jnp.sum(output * output, axis=1, keepdims=True)

    def total_over(buf, me, count, axis):
        copies = [
            links.send(buf.at[me], buf.at[me], {axis: mod(me + k, count)}) for k in range(1, count)
        ]
        for copy in copies:
            copy.wait_recv()
        total = buf[0]
        for n in range(1, count):
            total = total + buf[n]
        return total

    sums[t] = jnp.where(lane == 0, cross, jnp.where(lane == 1, squares, 0.0))
    both = total_over(sums, t, RING, "tensor")
    in_mean = keep[0][:, 0:1]
    cosine = both[:, 0:1] / width * lax.rsqrt((in_mean + EPS_COS) * (both[:, 1:2] / width + EPS_COS))
    local = jnp.sum(1.0 - cosine, axis=0, keepdims=True)
    totals[z] = jnp.broadcast_to(local, totals.shape[1:])
    grand[d] = total_over(totals, z, experts, "expert")
    score_ref[...] = total_over(grand, d, dp_count, "dp") / (tokens * experts * dp_count)
    links.drain()


def shards(hidden_in, expert_ids, ffn_gain, w_router, w_gate, w_up, w_down):
    tokens, width = hidden_in.shape[1:]
    top = expert_ids.shape[2]
    experts = lax.axis_size("expert")
    hidden = w_gate.shape[2]
    cap = max(2, 9 * tokens * top // (8 * experts))
    share = width // RING
    lanes = share // RING
    rows = experts * cap
    piece = (experts, MAIN, share + 128)
    vmem = pl.BlockSpec(memory_space=pltpu.VMEM)
    hbm = pl.BlockSpec(memory_space=pl.ANY)
    scratch = lambda shape, kind: pltpu.VMEM(shape, kind)
    copies = 160
    blocks = (RING, 2, RING, 2, rows, lanes)
    out, score = pl.pallas_call(
        functools.partial(kernel, (experts, cap)),
        out_shape=(
            jax.ShapeDtypeStruct((tokens, share), BF),
            jax.ShapeDtypeStruct((8, 128), F32),
        ),
        in_specs=[vmem] * 4 + [hbm] * 3,
        out_specs=(vmem, vmem),
        scratch_shapes=[
            scratch((width // lanes, lanes, hidden), BF),
            scratch((width // lanes, lanes, hidden), BF),
            scratch((hidden, width), BF),
            scratch((tokens, width), BF),
            scratch((8, tokens, 128), F32),
            scratch(piece, BF),
            scratch(piece, BF),
            scratch(piece, BF),
            scratch(piece, BF),
            scratch(blocks, BF),
            scratch(blocks, BF),
            scratch((RING, 2 * rows, hidden), F32),
            scratch((RING, 2 * rows, hidden), F32),
            scratch((RING, 2 * rows, hidden), BF),
            scratch(blocks, BF),
            scratch(blocks, BF),
            scratch((RING, 2, RING, rows, lanes), BF),
            scratch((RING, 2, RING, rows, lanes), BF),
            scratch((6, RING, rows, lanes), BF),
            scratch((6, RING, rows, lanes), BF),
            scratch((RING, 2, rows, lanes), BF),
            scratch((RING, 2, rows, lanes), BF),
            scratch((6, rows, lanes), BF),
            scratch((6, rows, lanes), BF),
            scratch((RING, rows, lanes), BF),
            scratch((RING, tokens, 128), F32),
            scratch((experts, 8, 128), F32),
            scratch((2 * RING, 8, 128), F32),
            pltpu.SemaphoreType.DMA((copies,)),
            pltpu.SemaphoreType.DMA((copies,)),
            pltpu.SemaphoreType.DMA((3,)),
        ],
        compiler_params=pltpu.CompilerParams(
            collective_id=0, has_side_effects=True, vmem_limit_bytes=67043328
        ),
        name="layer",
    )(
        hidden_in.reshape(tokens, width),
        expert_ids.reshape(tokens, top),
        ffn_gain.reshape(1, width),
        w_router,
        w_gate.reshape(width // lanes, lanes, hidden),
        w_up.reshape(width // lanes, lanes, hidden),
        w_down.reshape(hidden, width),
    )
    return out.reshape(1, tokens, share), score[0, 0]


def solution(mesh):
    return jax.shard_map(
        shards,
        mesh=mesh,
        in_specs=(
            P("dp", "expert", None),
            P("dp", "expert", None),
            P(),
            P(),
            P("expert", None, ("tensor", "dp")),
            P("expert", None, ("tensor", "dp")),
            P("expert", ("tensor", "dp"), None),
        ),
        out_specs=(P("dp", "expert", "tensor"), P()),
        check_vma=False,
    )
```

time: 367 us -> 139 us (0.38)
  waiting for transfers between devices: 186 us -> 0 us
  Pallas kernels: 0 us -> 119 us
  blocking collectives: 72.2 us -> 0 us
  matrix products: 34.1 us -> 0 us
  local copies, waits for them, and re-layouts: 43.7 us -> 19.3 us
  between operations: 16 us -> 0.64 us
  other arithmetic: 7.32 us -> 0 us
  starting transfers between devices: 6.92 us -> 0 us
    reduce_scatter x1 -> x0, waiting for transfers between devices: 126 us -> none  [shards(): lax.psum_scatter(terms.reshape(tensor_count * replica_count, expert_count...]
    pallas_call x0 -> x1, Pallas kernels: none -> 119 us  [shards(): pl.pallas_call(functools.partial(kernel, (experts, cap)), out_shape=(jax....]
    all_to_all x3 -> x0, blocking collectives: 72.2 us -> none  [the longest x1 47.4 us: shards(): lax.all_to_all(outgoing, 'expert', split_axis=0, concat_axis=0, tiled=True)]
    all_gather x1 -> x0, waiting for transfers between devices: 47.9 us -> none  [shards(): pieces = lax.all_gather(arrived, 'dp', axis=0, tiled=True)]
    dot_general x6 -> x0, matrix products: 34.1 us -> none  [the longest x1 12.1 us: shards(): jnp.einsum('snlcf,lftq->tsnlcq', activated, down_blocks, preferred_elemen...]
    transpose x1 -> x0, local copies, waits for them, and re-layouts: 21.7 us -> none  [shards(): jnp.einsum('snlcf,lftq->tsnlcq', activated, down_blocks, preferred_elemen...]
    unnamed x15 -> x4, local copies, waits for them, and re-layouts: 1.8 us -> 16.7 us
    all_to_all x1 -> x0, waiting for transfers between devices: 11.7 us -> none  [shards(): lax.all_to_all(summed[0].astype(jnp.bfloat16), 'expert', split_axis=0, co...]
  transfers between devices with their start and end apart: 3 -> 0, of which waited for: 3 -> 0; matrix products, arithmetic and copies ran while one was open for 2% -> 0% of each run, Pallas kernels for 0% -> 0%
where the time goes in v1:
time: 139 us
  Pallas kernels  119 us (86%)
  local copies, waits for them, and re-layouts  19.3 us (14%)
    pallas_call x1, Pallas kernels, shards(): pl.pallas_call(functools.partial(kernel, (experts, cap)), out_shape=(jax....  119 us
    unnamed x4, local copies, waits for them, and re-layouts  16.7 us

profile of v1, /device:TPU:1, one launch (start us, length us, event | category | flops | bytes accessed | tf_op | source)
XLA Modules:
  0.0 138.8 jit_solution(11641322489663579019)
XLA Ops:
  0.6 1.4 copy.11.ids_ref
  2.0 2.2 %copy.12.router_ref = bf16[4096,8]{1,0:T(8,128)(2,1)} copy(bf16[4096,8]{0,1:T(8,128)(2,1)} %param.10) | data formatting | bytes 131072 | tf_op args[3]
  4.3 6.4 %copy.9 = bf16[1,4096,448]{2,1,0:T(8,128)(2,1)} copy(bf16[1,4096,448]{1,2,0:T(8,128)(2,1)} %param.11) | data formatting | bytes 7340032 | tf_op args[4]
  10.7 6.5 %copy.10 = bf16[1,4096,448]{2,1,0:T(8,128)(2,1)} copy(bf16[1,4096,448]{1,2,0:T(8,128)(2,1)} %param.12) | data formatting | bytes 7340032 | tf_op args[5]
  17.1 118.9 %layer.1 = (bf16[64,1024]{1,0:T(8,128)(2,1)}, f32[8,128]{1,0:T(8,128)}) custom-call(bf16[64,4096]{1,0:T(8,128)(2,1)} %bitcast.11, s32[64,2]{1,0:T(8,128)} %copy.11.ids_ref, f32[1,4096]{1,0:T(1,128)} %bitcast.13, bf16[4096,8]{1,0:T(8,128)(2,1)} %copy.12.router_ref, bf16[16,256,448]{2,1,0:T(8,128)(2,1)} %bitcast.8, bf16[16,256,448]{2,1,0:T(8,128)(2,1)} %bitcast.9, ...), custom_call_target="tpu_custom_call" | custom-call | tf_op jit(solution)/shard_map/layer/pallas_call | solution.py:463
  136.0 1.2 slice.3
  137.2 1.6 %copy.14 = bf16[1,64,1024]{2,1,0:T(8,128)(2,1)} copy(bf16[1,64,1024]{2,1,0:T(8,128)(2,1)} %bitcast.12) | data formatting | bytes 262144

commit v2 on v1

v2 whole, which is shorter than its diff:
```python
import functools

import jax
import jax.numpy as jnp
from jax import lax
from jax.experimental import pallas as pl
from jax.experimental.pallas import tpu as pltpu
from jax.sharding import PartitionSpec as P

EPS_NORM = 1e-05
EPS_COS = 1e-06
BF = jnp.bfloat16
F32 = jnp.float32
RING = 4
SENDS = 64
MAIN = 16


class Links:
    def __init__(self, send_sems, recv_sems):
        self.send_sems, self.recv_sems, self.groups, self.started = send_sems, recv_sems, 0, []

    def group(self):
        self.groups += 1
        return self.groups - 1

    def send(self, src, dst, device, group=None):
        n = len(self.started)
        if n >= SENDS:
            self.started[n - SENDS].wait_send()
        copy = pltpu.make_async_remote_copy(
            src_ref=src,
            dst_ref=dst,
            send_sem=self.send_sems.at[n % SENDS],
            recv_sem=self.recv_sems.at[self.group() if group is None else group],
            device_id=device,
            device_id_type=pl.DeviceIdType.MESH,
        )
        copy.start()
        self.started.append(copy)
        return copy

    def arrived(self, group, whole, device):
        pltpu.make_async_remote_copy(
            src_ref=whole,
            dst_ref=whole,
            send_sem=self.send_sems.at[0],
            recv_sem=self.recv_sems.at[group],
            device_id=device,
            device_id_type=pl.DeviceIdType.MESH,
        ).wait_recv()

    def drain(self):
        for copy in self.started[-SENDS:]:
            copy.wait_send()


def mod(value, n):
    return lax.rem(value + 2 * n, n)


def dot(a, b):
    return jnp.dot(a, b, preferred_element_type=F32)


def dot_rows(a, b):
    return lax.dot_general(a, b, (((1,), (1,)), ((), ())), preferred_element_type=F32)


def onehot(mask):
    return jnp.where(mask, 1.0, 0.0).astype(BF)


def kernel(
    sizes,
    h_hbm, ids_hbm, gain_hbm, router_hbm, wg_hbm, wu_hbm, wd_hbm,
    out_hbm, score_ref,
    h_ref, ids_ref, gain_ref, router_ref, out_ref,
    wg, wu, wd, normed, keep, sent, got, back_sent, back,
    xa, xb, ga, ua, act, pa, pb, qa, qb, ra, rb, ta, tb, sa, sb, res,
    sums, totals, grand,
    send_sems, recv_sems, weight_sems,
):
    experts, cap = sizes
    tokens, width = h_hbm.shape
    share = width // RING
    lanes = share // RING
    rows = experts * cap
    spread_rows = experts * MAIN
    per_lane = MAIN // 2
    z = lax.axis_index("expert")
    t = lax.axis_index("tensor")
    d = lax.axis_index("dp")
    x, c = d // 2, lax.rem(d, 2)
    other = 1 - c
    x_of = lambda pos: {"dp": pos * 2 + c}
    y_of = lambda pos: {"tensor": pos}
    partner = {"dp": x * 2 + other}
    dp_count = RING * 2

    barrier = pltpu.get_barrier_semaphore()
    peers = (
        [{"expert": mod(z + k, experts)} for k in range(1, experts)]
        + [{"tensor": mod(t + k, RING)} for k in range(1, RING)]
        + [{"dp": mod(d + k, dp_count)} for k in range(1, dp_count)]
    )
    for peer in peers:
        pl.semaphore_signal(barrier, inc=1, device_id=peer, device_id_type=pl.DeviceIdType.MESH)

    weights = [
        pltpu.make_async_copy(src, dst, weight_sems.at[n])
        for n, (src, dst) in enumerate(
            (
                (wg_hbm, wg), (wu_hbm, wu), (wd_hbm, wd),
                (h_hbm, h_ref), (ids_hbm, ids_ref), (gain_hbm, gain_ref), (router_hbm, router_ref),
            )
        )
    ]
    for copy in weights[3:] + weights[:3]:
        copy.start()
    for copy in weights[3:]:
        copy.wait()

    token_rows = h_ref[...].astype(F32)
    in_squares = jnp.sum(token_rows * token_rows, axis=1, keepdims=True) / width
    normed[...] = (token_rows * lax.rsqrt(in_squares + EPS_NORM) * gain_ref[...]).astype(BF)
    logits = dot_rows(normed[...], router_ref[...])
    lane = lax.broadcasted_iota(jnp.int32, (tokens, 128), 1)
    lane_f = lane.astype(F32)
    ids = ids_ref[...].astype(F32)
    row_of = lax.broadcasted_iota(jnp.int32, (tokens, tokens), 0)
    lane_of = lax.broadcasted_iota(jnp.int32, (tokens, tokens), 1)
    first_f, second_f = (
        jnp.sum(jnp.where(row_of == lane_of, ids[n : n + 1], 0.0), axis=1, keepdims=True) for n in range(2)
    )
    is_first = jnp.where(lane_f == first_f, 1.0, 0.0)
    is_second = jnp.where(lane_f == second_f, 1.0, 0.0)
    spread = jnp.sum((is_first[:, :experts] - is_second[:, :experts]) * logits, axis=1, keepdims=True)
    gate_first = 1.0 / (1.0 + jnp.exp(-spread))
    gate_second = 1.0 / (1.0 + jnp.exp(spread))
    before = dot(onehot(lane_of < row_of), (is_first + is_second).astype(BF))
    kept = [in_squares, gate_first, gate_second]
    for chosen, mask in ((first_f, is_first), (second_f, is_second)):
        slot = jnp.sum(before * mask, axis=1, keepdims=True)
        place = chosen * MAIN + slot
        kept.append(jnp.where(slot < MAIN, place, -1.0))
        kept.append(jnp.where(slot < MAIN, -1000.0, place - MAIN))
    for n, column in enumerate(kept):
        keep[n] = jnp.broadcast_to(column, (tokens, 128))

    def chosen_masks(n, shift):
        return onehot(lane_f - shift == keep[n])

    main = (chosen_masks(3, 0.0) + chosen_masks(5, 0.0)).astype(F32).T.astype(BF)
    extra = jnp.zeros((spread_rows, 128), F32)
    for k in range(per_lane):
        picks = (chosen_masks(4, 2.0 * k) + chosen_masks(6, 2.0 * k)).astype(F32).T.astype(BF)
        block = normed[:, pl.ds(pl.multiple_of(t * share + k * 128, 128), 128)]
        extra = extra + dot(picks[:spread_rows], block)
    def spot(q):
        return (q // 2) * lanes + (q % 2) * (2 * lanes + 128)

    extra_at = 2 * lanes
    for q in range(RING):
        block = normed[:, pl.ds(pl.multiple_of(t * share + q * lanes, 128), lanes)]
        picked = dot(main[:spread_rows], block).astype(BF)
        sent[:, :, spot(q) : spot(q) + lanes] = picked.reshape(experts, MAIN, lanes)
    sent[:, :, extra_at : extra_at + 128] = extra.astype(BF).reshape(experts, MAIN, 128)

    ga[...] = jnp.zeros_like(ga)
    ua[...] = jnp.zeros_like(ua)
    pl.semaphore_wait(barrier, len(peers))
    links = Links(send_sems, recv_sems)

    def exchange(src, dst, begin, end):
        group = links.group()
        for k in sorted(range(1, experts), key=lambda k: -min(k, experts - k)):
            to = mod(z + k, experts)
            links.send(src.at[to, :, begin:end], dst.at[z, :, begin:end], {"expert": to}, group)
        dst[z, :, begin:end] = src[z, :, begin:end]
        return group, dst.at[: experts - 1, :, begin:end]

    def received(exchanged):
        links.arrived(*exchanged, partner)

    arriving = [exchange(sent, got, 0, extra_at + 128), exchange(sent, got, extra_at + 128, share + 128)]

    def placing(transposed):
        shape = (spread_rows, rows) if transposed else (rows, spread_rows)
        row = lax.broadcasted_iota(jnp.int32, shape, 1 if transposed else 0)
        place = lax.broadcasted_iota(jnp.int32, shape, 0 if transposed else 1)
        source, slot = place // MAIN, place % MAIN
        base = source * cap
        fits = (MAIN + slot % 2) < cap
        extras = [
            onehot((row == base + MAIN + slot % 2) & (slot // 2 == k) & fits) for k in range(per_lane)
        ]
        return onehot((row == base + slot) & (slot < cap)), extras

    put, put_extra = placing(False)

    def compact(j):
        extras = got[:, :, extra_at : extra_at + 128].reshape(spread_rows, 128)
        for q in (j, 2 + j):
            block = dot(put, got[:, :, spot(q) : spot(q) + lanes].reshape(spread_rows, lanes))
            halves = [dot(put_extra[k], extras) for k in range(q * lanes // 128, (q + 1) * lanes // 128)]
            block = (block + jnp.concatenate(halves, axis=1)).astype(BF)
            if q < 2:
                xa[x, j, t, c] = block
            else:
                xb[t, j, x, c] = block

    half = lanes // 2

    def part_of(h):
        return pl.ds(h * half, half)

    class Gather:
        def __init__(self, view, block, me, device_of):
            self.view, self.block = view, block
            self.left, self.right, self.far = mod(me - 1, RING), mod(me + 1, RING), mod(me + 2, RING)
            self.to_left, self.to_right = device_of(self.left), device_of(self.right)
            send = lambda pos, h, to: links.send(view(pos, h), view(pos, h), to)
            self.from_left = [send(me, 0, self.to_right)]
            self.from_right = [send(me, 1, self.to_left)]
            self.from_left.append(send(me, 1, self.to_right))
            self.from_right.append(send(me, 0, self.to_left))

        def pass_on(self):
            self.from_left[0].wait_recv()
            self.pass_halves(self.from_right[0].wait_recv)

        def pass_halves(self, wait_other):
            self.far_group = links.group()
            left = self.view(self.left, 0)
            links.send(left, left, self.to_right, self.far_group)
            wait_other()
            right = self.view(self.right, 1)
            links.send(right, right, self.to_left, self.far_group)

        def wait_left(self):
            self.from_left[1].wait_recv()

        def wait_right(self):
            self.from_right[1].wait_recv()

        def wait_far(self):
            links.arrived(self.far_group, self.block(self.far), self.to_left)

    class PiecewiseGather(Gather):
        def __init__(self, view, block, piece, me, device_of, short):
            self.view, self.block, self.piece, self.me = view, block, piece, me
            self.left, self.right, self.far = mod(me - 1, RING), mod(me + 1, RING), mod(me + 2, RING)
            self.to_left, self.to_right = device_of(self.left), device_of(self.right)
            self.order = (mod(short, RING), mod(short - 1, RING), mod(short + 1, RING), mod(short + 2, RING))
            self.right_going = links.group(), links.group()
            self.left_going = links.group(), links.group()

        def feed(self, n):
            for turn in range(2):
                for h, going, to in (
                    (turn, self.right_going, self.to_right),
                    (1 - turn, self.left_going, self.to_left),
                ):
                    block = self.piece(self.me, h, self.order[n])
                    links.send(block, block, to, going[h])

        def arrived(self, going, pos, h):
            links.arrived(going[h], self.view(pos, h), self.to_left)

        def pass_on(self):
            self.arrived(self.right_going, self.left, 0)
            self.pass_halves(lambda: self.arrived(self.left_going, self.right, 1))

        def wait_left(self):
            self.arrived(self.right_going, self.left, 1)

        def wait_right(self):
            self.arrived(self.left_going, self.right, 0)

    def small_gathers(j):
        return (
            Gather(lambda pos, h: xa.at[x, j, pos, c, :, part_of(h)], lambda pos: xa.at[x, j, pos, c], t, y_of),
            Gather(lambda pos, h: xb.at[t, j, pos, c, :, part_of(h)], lambda pos: xb.at[t, j, pos, c], x, x_of),
        )

    def big_gathers(j):
        return (
            PiecewiseGather(
                lambda pos, h: xa.at[pos, j, :, c, :, part_of(h)],
                lambda pos: xa.at[pos, j, :, c],
                lambda pos, h, n: xa.at[pos, j, n, c, :, part_of(h)],
                x, x_of, t,
            ),
            PiecewiseGather(
                lambda pos, h: xb.at[pos, j, :, c, :, part_of(h)],
                lambda pos: xb.at[pos, j, :, c],
                lambda pos, h, n: xb.at[pos, j, n, c, :, part_of(h)],
                t, y_of, x,
            ),
        )

    def feed_own(longs):
        for long in longs:
            long.feed(0)

    def feed_sides(shorts, longs):
        for short, long in zip(shorts, longs):
            short.wait_left()
            long.feed(1)
            short.wait_right()
            long.feed(2)

    def feed_far(shorts, longs):
        for short, long in zip(shorts, longs):
            short.wait_far()
            long.feed(3)

    def pass_on(gathers):
        for gather in gathers:
            gather.pass_on()

    def share_core(buf, pos, j):
        return links.send(buf.at[pos, j, :, c], buf.at[pos, j, :, c], partner)

    m = 2 * rows

    def columns(w, n):
        return w[:, pl.ds(pl.multiple_of(n * lanes, 128), lanes)]

    def up_a(copy, pos, j):
        copy.wait_recv()

        tokens_in = jnp.concatenate([xa[pos, j, y].reshape(m, lanes) for y in range(RING)], axis=1)
        for w, acc in ((wg, ga), (wu, ua)):
            columns_in = jnp.concatenate([columns(w, y * RING + j) for y in range(RING)], axis=1)
            acc[pos] += dot_rows(tokens_in, columns_in)

    def up_b(copy, pos, j):
        copy.wait_recv()

        for w, acc in ((wg, ga), (wu, ua)):
            product = dot_rows(xb[pos, j].reshape(RING * m, lanes), columns(w, pos * RING + 2 + j))
            acc[...] += product.reshape(acc.shape)

    def share_sides(gathers, j):
        shared = []
        for gather, buf, unit in zip(gathers, (xa, xb), (up_a, up_b)):
            gather.wait_left()
            shared.append((unit, share_core(buf, gather.left, j), gather.left))
            gather.wait_right()
            shared.append((unit, share_core(buf, gather.right, j), gather.right))
        return shared

    def share_far(gathers, j):
        shared = []
        for gather, buf, unit in zip(gathers, (xa, xb), (up_a, up_b)):
            gather.wait_far()
            shared.append((unit, share_core(buf, gather.far, j), gather.far))
        return shared

    def run(shared, j):
        for unit, copy, pos in shared:
            unit(copy, pos, j)

    received(arriving[0])
    compact(0)
    small_0, big_0 = small_gathers(0), big_gathers(0)
    feed_own(big_0)
    pass_on(small_0)
    received(arriving[1])
    compact(1)
    small_1, big_1 = small_gathers(1), big_gathers(1)
    feed_sides(small_0, big_0)
    feed_far(small_0, big_0)
    own_0 = [(up_a, share_core(xa, x, 0), x), (up_b, share_core(xb, t, 0), t)]
    feed_own(big_1)
    pass_on(small_1)
    weights[0].wait()
    weights[1].wait()
    run(own_0, 0)
    feed_sides(small_1, big_1)
    feed_far(small_1, big_1)
    own_1 = [(up_a, share_core(xa, x, 1), x), (up_b, share_core(xb, t, 1), t)]
    pass_on(big_0)
    run(own_1, 1)
    sides_0 = share_sides(big_0, 0)
    run(sides_0, 0)
    pass_on(big_1)
    sides_1 = share_sides(big_1, 1)
    run(sides_1[:2], 1)
    far_0 = share_far(big_0, 0)
    run(sides_1[2:], 1)
    run(far_0[:1], 0)
    far_1 = share_far(big_1, 1)
    run(far_0[1:], 0)
    run(far_1, 1)

    weights[2].wait()

    @pl.loop(0, RING)
    def _(xp):
        gate = ga[xp]
        act[xp] = (gate / (1.0 + jnp.exp(-gate)) * ua[xp]).astype(BF)

    def down_a(pos, j):
        columns_in = jnp.concatenate([columns(wd, y * RING + j) for y in range(RING)], axis=1)
        product = dot(act[pos], columns_in).astype(BF)
        for y in range(RING):
            pa[pos, j, y] = product[:, y * lanes : (y + 1) * lanes].reshape(2, rows, lanes)

        return links.send(pa.at[pos, j, :, other], qa.at[pos, j], partner)

    def down_b(pos, j):
        product = dot(act[...].reshape(RING * m, act.shape[2]), columns(wd, pos * RING + 2 + j)).astype(BF)
        pb[pos, j] = product.reshape(RING, 2, rows, lanes)

        return links.send(pb.at[pos, j, :, other], qb.at[pos, j], partner)

    def add_pair(copy, part, came, pos, j):
        copy.wait_recv()

        @pl.loop(0, RING)
        def _(n):
            part[pos, j, n, c] = (part[pos, j, n, c].astype(F32) + came[pos, j, n].astype(F32)).astype(BF)

    class Scatter:
        def __init__(self, view, slots, me, device_of):
            self.view, self.slots, self.me = view, slots, me
            self.left, self.right, self.far = mod(me - 1, RING), mod(me + 1, RING), mod(me + 2, RING)
            self.to_left, self.to_right = device_of(self.left), device_of(self.right)

        def send_far(self):
            self.rightward = links.send(self.view(self.far, 0), self.slots.at[0], self.to_right)
            self.leftward = links.send(self.view(self.far, 1), self.slots.at[1], self.to_left)

            self.last_group = links.group()

        def send_right(self):
            links.send(self.view(self.right, 1), self.slots.at[2], self.to_right, self.last_group)

        def send_left(self):
            links.send(self.view(self.left, 0), self.slots.at[3], self.to_left, self.last_group)

        def send_sums(self, add):
            self.rightward.wait_recv()
            add(self.right, 0, self.slots.at[0])
            links.send(self.view(self.right, 0), self.slots.at[4], self.to_right, self.last_group)
            self.leftward.wait_recv()
            add(self.left, 1, self.slots.at[1])
            links.send(self.view(self.left, 1), self.slots.at[5], self.to_left, self.last_group)

        def wait(self):
            links.arrived(self.last_group, self.slots.at[2:6], self.to_left)

        def parts(self, h):
            return (self.slots.at[4], self.slots.at[3]) if h == 0 else (self.slots.at[2], self.slots.at[5])

    def big_a(j):
        return Scatter(lambda pos, h: pa.at[pos, j, :, c, :, part_of(h)], ra.at[j], x, x_of)

    def big_b(j):
        return Scatter(lambda pos, h: pb.at[pos, j, :, c, :, part_of(h)], rb.at[j], t, y_of)

    def adder(part, j):
        def add(pos, h, slot):
            @pl.loop(0, RING)
            def _(n):
                own = part[pos, j, n, c, :, part_of(h)].astype(F32)
                part[pos, j, n, c, :, part_of(h)] = (own + slot[n].astype(F32)).astype(BF)

        return add

    rs_a, rs_b = [big_a(0), big_a(1)], [big_b(0), big_b(1)]
    pair_a, pair_b = down_a(rs_a[0].far, 0), down_b(rs_b[0].far, 0)
    for j in range(2):
        one, two = rs_a[j], rs_b[j]
        add_pair(pair_a, pa, qa, one.far, j)
        one.send_far()
        pair_a = down_a(one.right, j)
        add_pair(pair_b, pb, qb, two.far, j)
        two.send_far()
        pair_b = down_b(two.right, j)
        add_pair(pair_a, pa, qa, one.right, j)
        one.send_right()
        pair_a = down_a(one.left, j)
        add_pair(pair_b, pb, qb, two.right, j)
        two.send_right()
        pair_b = down_b(two.left, j)
        add_pair(pair_a, pa, qa, one.left, j)
        one.send_left()
        pair_a = down_a(one.far, 1) if j == 0 else down_a(x, 0)
        add_pair(pair_b, pb, qb, two.left, j)
        two.send_left()
        pair_b = down_b(two.far, 1) if j == 0 else down_b(t, 0)
        if j == 0:
            one.send_sums(adder(pa, j))
            two.send_sums(adder(pb, j))
    own_a, own_b = down_a(x, 1), down_b(t, 1)
    add_pair(pair_a, pa, qa, x, 0)
    add_pair(pair_b, pb, qb, t, 0)

    def finish_big(scatter, part, total, me, j):
        scatter.wait()

        @pl.loop(0, RING)
        def _(n):
            for h in range(2):
                one, two = scatter.parts(h)
                value = part[me, j, n, c, :, part_of(h)].astype(F32)
                total[n, j, :, part_of(h)] = (value + one[n].astype(F32) + two[n].astype(F32)).astype(BF)

    def small_a(j):
        finish_big(rs_a[j], pa, ta, x, j)
        small = Scatter(lambda pos, h: ta.at[pos, j, :, part_of(h)], sa.at[j], t, y_of)
        small.send_far()
        small.send_right()
        small.send_left()
        return small

    def small_b(j):
        finish_big(rs_b[j], pb, tb, t, j)
        small = Scatter(lambda pos, h: tb.at[pos, j, :, part_of(h)], sb.at[j], x, x_of)
        small.send_far()
        small.send_right()
        small.send_left()
        return small

    def small_adder(total, j):
        def add(pos, h, slot):
            own = total[pos, j, :, part_of(h)].astype(F32)
            total[pos, j, :, part_of(h)] = (own + slot[...].astype(F32)).astype(BF)

        return add

    def finish_small(small, total, q, j):
        small.wait()
        for h in range(2):
            one, two = small.parts(h)
            value = total[small.me, j, :, part_of(h)].astype(F32)
            res[q, :, part_of(h)] = (value + one[...].astype(F32) + two[...].astype(F32)).astype(BF)

    take, take_extra = placing(True)

    def take_out(q):
        picked = dot(take, res[q]).astype(BF)
        back_sent[:, :, spot(q) : spot(q) + lanes] = picked.reshape(experts, MAIN, lanes)

    last_a, last_b = [small_a(0)], [small_b(0)]
    add_pair(own_a, pa, qa, x, 1)
    add_pair(own_b, pb, qb, t, 1)
    rs_a[1].send_sums(adder(pa, 1))
    rs_b[1].send_sums(adder(pb, 1))
    last_a[0].send_sums(small_adder(ta, 0))
    last_b[0].send_sums(small_adder(tb, 0))
    last_a.append(small_a(1))
    last_b.append(small_b(1))
    finish_small(last_a[0], ta, 0, 0)
    finish_small(last_b[0], tb, 2, 0)
    take_out(0)
    take_out(2)
    returning = [exchange(back_sent, back, 0, extra_at)]
    last_a[1].send_sums(small_adder(ta, 1))
    last_b[1].send_sums(small_adder(tb, 1))
    finish_small(last_a[1], ta, 1, 1)
    finish_small(last_b[1], tb, 3, 1)
    take_out(1)
    take_out(3)
    extra = jnp.zeros((spread_rows, 128), F32)
    for k in range(per_lane):
        q, at = k * 128 // lanes, k * 128 % lanes
        extra = extra + dot(take_extra[k], res[q, :, at : at + 128])
    back_sent[:, :, extra_at : extra_at + 128] = extra.astype(BF).reshape(experts, MAIN, 128)
    returning.append(exchange(back_sent, back, extra_at, share + 128))
    received(returning[0])
    received(returning[1])

    extras = back[:, :, extra_at : extra_at + 128].reshape(spread_rows, 128)
    cross = jnp.zeros((tokens, 1), F32)
    squares = jnp.zeros((tokens, 1), F32)
    for k in range(share // 128):
        at = spot(k * 128 // lanes) + k * 128 % lanes
        block = back[:, :, at : at + 128].reshape(spread_rows, 128)
        mixture = jnp.zeros((tokens, 128), F32)
        for gate, n in ((1, 3), (2, 5)):
            picked = dot(chosen_masks(n, 0.0)[:, :spread_rows], block)
            picked = picked + dot(chosen_masks(n + 1, 2.0 * k)[:, :spread_rows], extras)
            mixture = mixture + keep[gate] * picked
        own = h_ref[:, pl.ds(pl.multiple_of(t * share + k * 128, 128), 128)].astype(F32)
        output = (own + mixture).astype(BF)
        out_ref[:, k * 128 : (k + 1) * 128] = output
        output = output.astype(F32)
        cross = cross + jnp.sum(own * output, axis=1, keepdims=True)
        squares = squares + jnp.sum(output * output, axis=1, keepdims=True)

    out_copy = pltpu.make_async_copy(out_ref, out_hbm, weight_sems.at[7])
    out_copy.start()

    def total_over(buf, me, count, axis):
        group = links.group()
        for k in range(1, count):
            links.send(buf.at[me], buf.at[me], {axis: mod(me + k, count)}, group)
        links.arrived(group, buf.at[: count - 1], partner)
        total = buf[0]
        for n in range(1, count):
            total = total + buf[n]
        return total

    sums[t] = jnp.where(lane == 0, cross, jnp.where(lane == 1, squares, 0.0))
    both = total_over(sums, t, RING, "tensor")
    in_mean = keep[0][:, 0:1]
    cosine = both[:, 0:1] / width * lax.rsqrt((in_mean + EPS_COS) * (both[:, 1:2] / width + EPS_COS))
    local = jnp.sum(1.0 - cosine, axis=0, keepdims=True)
    totals[z] = jnp.broadcast_to(local, totals.shape[1:])
    grand[d] = total_over(totals, z, experts, "expert")
    score = total_over(grand, d, dp_count, "dp") / (tokens * experts * dp_count)
    score_ref[0, 0] = score[0, 0]
    out_copy.wait()
    links.drain()


def shards(hidden_in, expert_ids, ffn_gain, w_router, w_gate, w_up, w_down):
    tokens, width = hidden_in.shape[1:]
    top = expert_ids.shape[2]
    experts = lax.axis_size("expert")
    hidden = w_gate.shape[2]
    cap = max(2, 9 * tokens * top // (8 * experts))
    share = width // RING
    lanes = share // RING
    rows = experts * cap
    piece = (experts, MAIN, share + 128)
    hbm = pl.BlockSpec(memory_space=pl.ANY)
    scratch = lambda shape, kind: pltpu.VMEM(shape, kind)
    blocks = (RING, 2, RING, 2, rows, lanes)
    out, score = pl.pallas_call(
        functools.partial(kernel, (experts, cap)),
        out_shape=(
            jax.ShapeDtypeStruct((tokens, share), BF),
            jax.ShapeDtypeStruct((1, 1), F32),
        ),
        in_specs=[hbm] * 7,
        out_specs=(hbm, pl.BlockSpec(memory_space=pltpu.SMEM)),
        scratch_shapes=[
            scratch((tokens, width), BF),
            scratch((top, tokens), jnp.int32),
            scratch((1, width), F32),
            scratch((experts, width), BF),
            scratch((tokens, share), BF),
            scratch((hidden, width), BF),
            scratch((hidden, width), BF),
            scratch((hidden, width), BF),
            scratch((tokens, width), BF),
            scratch((8, tokens, 128), F32),
            scratch(piece, BF),
            scratch(piece, BF),
            scratch(piece, BF),
            scratch(piece, BF),
            scratch(blocks, BF),
            scratch(blocks, BF),
            scratch((RING, 2 * rows, hidden), F32),
            scratch((RING, 2 * rows, hidden), F32),
            scratch((RING, 2 * rows, hidden), BF),
            scratch(blocks, BF),
            scratch(blocks, BF),
            scratch((RING, 2, RING, rows, lanes), BF),
            scratch((RING, 2, RING, rows, lanes), BF),
            scratch((2, 6, RING, rows, lanes // 2), BF),
            scratch((2, 6, RING, rows, lanes // 2), BF),
            scratch((RING, 2, rows, lanes), BF),
            scratch((RING, 2, rows, lanes), BF),
            scratch((2, 6, rows, lanes // 2), BF),
            scratch((2, 6, rows, lanes // 2), BF),
            scratch((RING, rows, lanes), BF),
            scratch((RING, tokens, 128), F32),
            scratch((experts, 8, 128), F32),
            scratch((2 * RING, 8, 128), F32),
            pltpu.SemaphoreType.DMA((SENDS,)),
            pltpu.SemaphoreType.DMA((103,)),
            pltpu.SemaphoreType.DMA((8,)),
        ],
        compiler_params=pltpu.CompilerParams(
            collective_id=0, has_side_effects=True, vmem_limit_bytes=67043328
        ),
        name="layer",
    )(
        hidden_in.reshape(tokens, width),
        expert_ids.reshape(tokens, top).T,
        ffn_gain.reshape(1, width),
        w_router.T,
        w_gate.reshape(width, hidden).T,
        w_up.reshape(width, hidden).T,
        w_down.reshape(hidden, width),
    )
    return out.reshape(1, tokens, share), score[0, 0]


def solution(mesh):
    return jax.shard_map(
        shards,
        mesh=mesh,
        in_specs=(
            P("dp", "expert", None),
            P("dp", "expert", None),
            P(),
            P(),
            P("expert", None, ("tensor", "dp")),
            P("expert", None, ("tensor", "dp")),
            P("expert", ("tensor", "dp"), None),
        ),
        out_specs=(P("dp", "expert", "tensor"), P()),
        check_vma=False,
    )
```

time: 139 us -> 107 us (0.77)
  local copies, waits for them, and re-layouts: 19.3 us -> 1.57 us
  Pallas kernels: 119 us -> 103 us
  between operations: 0.64 us -> 2.45 us
    pallas_call x1, Pallas kernels: 119 us -> 103 us  [shards(): pl.pallas_call(functools.partial(kernel, (experts, cap)), out_shape=(jax....]
    unnamed x4 -> x1, local copies, waits for them, and re-layouts: 16.7 us -> 1.57 us
where the time goes in v2:
time: 107 us
  Pallas kernels  103 us (96%)
  between operations  2.45 us (2%)
  local copies, waits for them, and re-layouts  1.57 us (1%)
    pallas_call x1, Pallas kernels, shards(): pl.pallas_call(functools.partial(kernel, (experts, cap)), out_shape=(jax....  103 us

profile of v2, /device:TPU:1, one launch (start us, length us, event | category | flops | bytes accessed | tf_op | source)
XLA Modules:
  0.0 106.8 jit_solution(15834685722890763992)
XLA Ops:
  0.6 102.8 %layer.1 = (bf16[64,1024]{1,0:T(8,128)(2,1)}, f32[1,1]{1,0:T(1,128)}) custom-call(bf16[64,4096]{1,0:T(8,128)(2,1)} %bitcast.18, s32[2,64]{1,0:T(2,128)} %bitcast.22, f32[1,4096]{1,0:T(1,128)} %bitcast.21, bf16[8,4096]{1,0:T(8,128)(2,1)} %bitcast.20, bf16[448,4096]{1,0:T(8,128)(2,1)} %bitcast.15, bf16[448,4096]{1,0:T(8,128)(2,1)} %bitcast.16, ...), custom_call_target="tpu_custom_call" | custom-call | tf_op jit(solution)/shard_map/layer/pallas_call | solution.py:635
  103.4 1.6 %copy.11 = bf16[1,64,1024]{2,1,0:T(8,128)(2,1)} copy(bf16[1,64,1024]{2,1,0:T(8,128)(2,1)} %bitcast.19) | data formatting | bytes 262144

commit v3 on v2

--- a/solution.py
+++ b/solution.py
@@ -14,6 +14,8 @@
 RING = 4
 SENDS = 64
 MAIN = 16
+SLOTS = (10, 8)
+WIDE = 8
 
 
 class Links:
@@ -76,18 +78,18 @@
     h_hbm, ids_hbm, gain_hbm, router_hbm, wg_hbm, wu_hbm, wd_hbm,
     out_hbm, score_ref,
     h_ref, ids_ref, gain_ref, router_ref, out_ref,
-    wg, wu, wd, normed, keep, sent, got, back_sent, back,
-    xa, xb, ga, ua, act, pa, pb, qa, qb, ra, rb, ta, tb, sa, sb, res,
-    sums, totals, grand,
-    send_sems, recv_sems, weight_sems,
+    wg, wu, wd, turned_g, turned_u, normed, keep, sent, got, back_sent, back,
+    *buffers,
 ):
+    *buffers, mixed, sums, totals, grand, send_sems, recv_sems, weight_sems = buffers
+    xa, xb, ga, ua, act, pa, pb, qa, qb, ra, rb, ta, tb, sa, sb, ea, eb = zip(buffers[::2], buffers[1::2])
     experts, cap = sizes
     tokens, width = h_hbm.shape
     share = width // RING
-    lanes = share // RING
-    rows = experts * cap
+    lanes = share // 2
+    rows = [experts * n for n in SLOTS]
     spread_rows = experts * MAIN
-    per_lane = MAIN // 2
+    blocks = share // 128
     z = lax.axis_index("expert")
     t = lax.axis_index("tensor")
     d = lax.axis_index("dp")
@@ -142,33 +144,37 @@
     kept = [in_squares, gate_first, gate_second]
     for chosen, mask in ((first_f, is_first), (second_f, is_second)):
         slot = jnp.sum(before * mask, axis=1, keepdims=True)
-        place = chosen * MAIN + slot
-        kept.append(jnp.where(slot < MAIN, place, -1.0))
-        kept.append(jnp.where(slot < MAIN, -1000.0, place - MAIN))
+        place = chosen * MAIN
+        late = slot - SLOTS[0]
+        kept.append(jnp.where(slot < WIDE, place + 2.0 * slot, -1000.0))
+        kept.append(jnp.where((slot >= WIDE) & (late < 0.0), place + slot - WIDE, -1000.0))
+        kept.append(jnp.where(late >= 0.0, place + 2.0 * late, -1000.0))
     for n, column in enumerate(kept):
         keep[n] = jnp.broadcast_to(column, (tokens, 128))
 
     def chosen_masks(n, shift):
         return onehot(lane_f - shift == keep[n])
 
-    main = (chosen_masks(3, 0.0) + chosen_masks(5, 0.0)).astype(F32).T.astype(BF)
-    extra = jnp.zeros((spread_rows, 128), F32)
-    for k in range(per_lane):
-        picks = (chosen_masks(4, 2.0 * k) + chosen_masks(6, 2.0 * k)).astype(F32).T.astype(BF)
-        block = normed[:, pl.ds(pl.multiple_of(t * share + k * 128, 128), 128)]
-        extra = extra + dot(picks[:spread_rows], block)
-    def spot(q):
-        return (q // 2) * lanes + (q % 2) * (2 * lanes + 128)
-
-    extra_at = 2 * lanes
-    for q in range(RING):
-        block = normed[:, pl.ds(pl.multiple_of(t * share + q * lanes, 128), lanes)]
-        picked = dot(main[:spread_rows], block).astype(BF)
-        sent[:, :, spot(q) : spot(q) + lanes] = picked.reshape(experts, MAIN, lanes)
+    extra_at = lanes
+    starts, ends = (0, lanes + 128), (lanes + 128, 2 * lanes + 128)
+
+    def picks(n, shift):
+        return (chosen_masks(n, shift) + chosen_masks(n + 3, shift)).astype(F32).T.astype(BF)[:spread_rows]
+
+    def own_lanes(k):
+        return pl.ds(pl.multiple_of(t * share + k * 128, 128), 128)
+
+    for j in range(2):
+        select = [picks(3 + 2 * j, float(b)) for b in range(2)]
+        for p in range(blocks // 2):
+            picked = sum(dot(select[b], normed[:, own_lanes(2 * p + b)]) for b in range(2))
+            at = starts[j] + p * 128
+            sent[:, :, at : at + 128] = picked.astype(BF).reshape(experts, MAIN, 128)
+    extra = sum(dot(picks(4, 2.0 * k), normed[:, own_lanes(k)]) for k in range(blocks))
     sent[:, :, extra_at : extra_at + 128] = extra.astype(BF).reshape(experts, MAIN, 128)
 
-    ga[...] = jnp.zeros_like(ga)
-    ua[...] = jnp.zeros_like(ua)
+    for acc in ga + ua:
+        acc[...] = jnp.zeros_like(acc)
     pl.semaphore_wait(barrier, len(peers))
     links = Links(send_sems, recv_sems)
 
@@ -183,32 +189,31 @@
     def received(exchanged):
         links.arrived(*exchanged, partner)
 
-    arriving = [exchange(sent, got, 0, extra_at + 128), exchange(sent, got, extra_at + 128, share + 128)]
-
-    def placing(transposed):
-        shape = (spread_rows, rows) if transposed else (rows, spread_rows)
+    arriving = [exchange(sent, got, starts[j], ends[j]) for j in range(2)]
+
+    def placing(j, transposed):
+        shape = (spread_rows, rows[j]) if transposed else (rows[j], spread_rows)
         row = lax.broadcasted_iota(jnp.int32, shape, 1 if transposed else 0)
         place = lax.broadcasted_iota(jnp.int32, shape, 0 if transposed else 1)
-        source, slot = place // MAIN, place % MAIN
-        base = source * cap
-        fits = (MAIN + slot % 2) < cap
-        extras = [
-            onehot((row == base + MAIN + slot % 2) & (slot // 2 == k) & fits) for k in range(per_lane)
-        ]
-        return onehot((row == base + slot) & (slot < cap)), extras
-
-    put, put_extra = placing(False)
+        base, within = place // MAIN * SLOTS[j], place % MAIN
+        wide = [onehot((row == base + within // 2) & (within % 2 == b)) for b in range(2)]
+        extras = [onehot((row == base + WIDE + within % 2) & (within // 2 == k)) for k in range(blocks)]
+        return wide, extras
 
     def compact(j):
+        wide, put_extra = placing(j, False)
+        pieces = got[:, :, starts[j] : starts[j] + lanes].reshape(spread_rows, lanes)
+        both = [dot(wide[b], pieces) for b in range(2)]
         extras = got[:, :, extra_at : extra_at + 128].reshape(spread_rows, 128)
-        for q in (j, 2 + j):
-            block = dot(put, got[:, :, spot(q) : spot(q) + lanes].reshape(spread_rows, lanes))
-            halves = [dot(put_extra[k], extras) for k in range(q * lanes // 128, (q + 1) * lanes // 128)]
-            block = (block + jnp.concatenate(halves, axis=1)).astype(BF)
-            if q < 2:
-                xa[x, j, t, c] = block
+        for k in range(blocks):
+            value = both[k % 2][:, k // 2 * 128 : (k // 2 + 1) * 128]
+            if j == 0:
+                value = value + dot(put_extra[k], extras)
+            at = k * 128 % lanes
+            if k * 128 < lanes:
+                xa[j][x, t, c, :, at : at + 128] = value.astype(BF)
             else:
-                xb[t, j, x, c] = block
+                xb[j][t, x, c, :, at : at + 128] = value.astype(BF)
 
     half = lanes // 2
 
@@ -280,22 +285,26 @@
 
     def small_gathers(j):
         return (
-            Gather(lambda pos, h: xa.at[x, j, pos, c, :, part_of(h)], lambda pos: xa.at[x, j, pos, c], t, y_of),
-            Gather(lambda pos, h: xb.at[t, j, pos, c, :, part_of(h)], lambda pos: xb.at[t, j, pos, c], x, x_of),
+            Gather(
+                lambda pos, h: xa[j].at[x, pos, c, :, part_of(h)], lambda pos: xa[j].at[x, pos, c], t, y_of
+            ),
+            Gather(
+                lambda pos, h: xb[j].at[t, pos, c, :, part_of(h)], lambda pos: xb[j].at[t, pos, c], x, x_of
+            ),
         )
 
     def big_gathers(j):
         return (
             PiecewiseGather(
-                lambda pos, h: xa.at[pos, j, :, c, :, part_of(h)],
-                lambda pos: xa.at[pos, j, :, c],
-                lambda pos, h, n: xa.at[pos, j, n, c, :, part_of(h)],
+                lambda pos, h: xa[j].at[pos, :, c, :, part_of(h)],
+                lambda pos: xa[j].at[pos, :, c],
+                lambda pos, h, n: xa[j].at[pos, n, c, :, part_of(h)],
                 x, x_of, t,
             ),
             PiecewiseGather(
-                lambda pos, h: xb.at[pos, j, :, c, :, part_of(h)],
-                lambda pos: xb.at[pos, j, :, c],
-                lambda pos, h, n: xb.at[pos, j, n, c, :, part_of(h)],
+                lambda pos, h: xb[j].at[pos, :, c, :, part_of(h)],
+                lambda pos: xb[j].at[pos, :, c],
+                lambda pos, h, n: xb[j].at[pos, n, c, :, part_of(h)],
                 t, y_of, x,
             ),
         )
@@ -321,26 +330,32 @@
             gather.pass_on()
 
     def share_core(buf, pos, j):
-        return links.send(buf.at[pos, j, :, c], buf.at[pos, j, :, c], partner)
-
-    m = 2 * rows
-
-    def columns(w, n):
-        return w[:, pl.ds(pl.multiple_of(n * lanes, 128), lanes)]
+        return links.send(buf[j].at[pos, :, c], buf[j].at[pos, :, c], partner)
+
+    def turn(n):
+        @pl.loop(0, RING)
+        def _(k):
+            at = pl.multiple_of(n * share + k * (share // RING), 128)
+            for w, turned in ((wg, turned_g), (wu, turned_u)):
+                turned[pl.ds(at, share // RING), :] = w[:, pl.ds(at, share // RING)].T
+
+    def up_rows(w, n, second):
+        return w[pl.ds(pl.multiple_of(n * share + second * lanes, 128), lanes), :]
+
+    def columns(w, n, second):
+        return w[:, pl.ds(pl.multiple_of(n * share + second * lanes, 128), lanes)]
 
     def up_a(copy, pos, j):
         copy.wait_recv()
-
-        tokens_in = jnp.concatenate([xa[pos, j, y].reshape(m, lanes) for y in range(RING)], axis=1)
-        for w, acc in ((wg, ga), (wu, ua)):
-            columns_in = jnp.concatenate([columns(w, y * RING + j) for y in range(RING)], axis=1)
-            acc[pos] += dot_rows(tokens_in, columns_in)
+        tokens_in = jnp.concatenate([xa[j][pos, y].reshape(2 * rows[j], lanes) for y in range(RING)], axis=1)
+        for w, acc in ((turned_g, ga[j]), (turned_u, ua[j])):
+            rows_in = jnp.concatenate([up_rows(w, y, 0) for y in range(RING)], axis=0)
+            acc[pos] += dot(tokens_in, rows_in)
 
     def up_b(copy, pos, j):
         copy.wait_recv()
-
-        for w, acc in ((wg, ga), (wu, ua)):
-            product = dot_rows(xb[pos, j].reshape(RING * m, lanes), columns(w, pos * RING + 2 + j))
+        for w, acc in ((turned_g, ga[j]), (turned_u, ua[j])):
+            product = dot(xb[j][pos].reshape(2 * RING * rows[j], lanes), up_rows(w, pos, 1))
             acc[...] += product.reshape(acc.shape)
 
     def share_sides(gathers, j):
@@ -363,66 +378,62 @@
         for unit, copy, pos in shared:
             unit(copy, pos, j)
 
+    weights[0].wait()
+    weights[1].wait()
+    turn(0)
+    turn(1)
     received(arriving[0])
     compact(0)
     small_0, big_0 = small_gathers(0), big_gathers(0)
     feed_own(big_0)
+    turn(2)
     pass_on(small_0)
     received(arriving[1])
     compact(1)
-    small_1, big_1 = small_gathers(1), big_gathers(1)
+    small_1 = small_gathers(1)
     feed_sides(small_0, big_0)
     feed_far(small_0, big_0)
     own_0 = [(up_a, share_core(xa, x, 0), x), (up_b, share_core(xb, t, 0), t)]
+    pass_on(small_1)
+    turn(3)
+    run(own_0, 0)
+    pass_on(big_0)
+    big_1 = big_gathers(1)
     feed_own(big_1)
-    pass_on(small_1)
-    weights[0].wait()
-    weights[1].wait()
-    run(own_0, 0)
     feed_sides(small_1, big_1)
     feed_far(small_1, big_1)
     own_1 = [(up_a, share_core(xa, x, 1), x), (up_b, share_core(xb, t, 1), t)]
-    pass_on(big_0)
+    sides_0 = share_sides(big_0, 0)
     run(own_1, 1)
-    sides_0 = share_sides(big_0, 0)
-    run(sides_0, 0)
+    run(sides_0[:2], 0)
+    far_0 = share_far(big_0, 0)
+    run(sides_0[2:], 0)
     pass_on(big_1)
-    sides_1 = share_sides(big_1, 1)
-    run(sides_1[:2], 1)
-    far_0 = share_far(big_0, 0)
-    run(sides_1[2:], 1)
-    run(far_0[:1], 0)
-    far_1 = share_far(big_1, 1)
-    run(far_0[1:], 0)
-    run(far_1, 1)
-
-    weights[2].wait()
-
-    @pl.loop(0, RING)
-    def _(xp):
-        gate = ga[xp]
-        act[xp] = (gate / (1.0 + jnp.exp(-gate)) * ua[xp]).astype(BF)
+    run(far_0, 0)
+
+    def activate(pos, j):
+        gate = ga[j][pos]
+        act[j][pos] = (gate / (1.0 + jnp.exp(-gate)) * ua[j][pos]).astype(BF)
 
     def down_a(pos, j):
-        columns_in = jnp.concatenate([columns(wd, y * RING + j) for y in range(RING)], axis=1)
-        product = dot(act[pos], columns_in).astype(BF)
+        columns_in = jnp.concatenate([columns(wd, y, 0) for y in range(RING)], axis=1)
+        product = dot(act[j][pos], columns_in).astype(BF)
         for y in range(RING):
-            pa[pos, j, y] = product[:, y * lanes : (y + 1) * lanes].reshape(2, rows, lanes)
-
-        return links.send(pa.at[pos, j, :, other], qa.at[pos, j], partner)
+            pa[j][pos, y] = product[:, y * lanes : (y + 1) * lanes].reshape(2, rows[j], lanes)
+        return links.send(pa[j].at[pos, :, other], qa[j].at[pos], partner)
 
     def down_b(pos, j):
-        product = dot(act[...].reshape(RING * m, act.shape[2]), columns(wd, pos * RING + 2 + j)).astype(BF)
-        pb[pos, j] = product.reshape(RING, 2, rows, lanes)
-
-        return links.send(pb.at[pos, j, :, other], qb.at[pos, j], partner)
+        tokens_in = act[j][...].reshape(2 * RING * rows[j], act[j].shape[2])
+        product = dot(tokens_in, columns(wd, pos, 1)).astype(BF)
+        pb[j][pos] = product.reshape(RING, 2, rows[j], lanes)
+        return links.send(pb[j].at[pos, :, other], qb[j].at[pos], partner)
 
     def add_pair(copy, part, came, pos, j):
         copy.wait_recv()
 
         @pl.loop(0, RING)
         def _(n):
-            part[pos, j, n, c] = (part[pos, j, n, c].astype(F32) + came[pos, j, n].astype(F32)).astype(BF)
+            part[j][pos, n, c] = (part[j][pos, n, c].astype(F32) + came[j][pos, n].astype(F32)).astype(BF)
 
     class Scatter:
         def __init__(self, view, slots, me, device_of):
@@ -456,25 +467,28 @@
         def parts(self, h):
             return (self.slots.at[4], self.slots.at[3]) if h == 0 else (self.slots.at[2], self.slots.at[5])
 
-    def big_a(j):
-        return Scatter(lambda pos, h: pa.at[pos, j, :, c, :, part_of(h)], ra.at[j], x, x_of)
-
-    def big_b(j):
-        return Scatter(lambda pos, h: pb.at[pos, j, :, c, :, part_of(h)], rb.at[j], t, y_of)
-
     def adder(part, j):
         def add(pos, h, slot):
             @pl.loop(0, RING)
             def _(n):
-                own = part[pos, j, n, c, :, part_of(h)].astype(F32)
-                part[pos, j, n, c, :, part_of(h)] = (own + slot[n].astype(F32)).astype(BF)
+                own = part[j][pos, n, c, :, part_of(h)].astype(F32)
+                part[j][pos, n, c, :, part_of(h)] = (own + slot[n].astype(F32)).astype(BF)
 
         return add
 
-    rs_a, rs_b = [big_a(0), big_a(1)], [big_b(0), big_b(1)]
-    pair_a, pair_b = down_a(rs_a[0].far, 0), down_b(rs_b[0].far, 0)
-    for j in range(2):
+    rs_a = [Scatter(lambda pos, h, j=j: pa[j].at[pos, :, c, :, part_of(h)], ra[j], x, x_of) for j in range(2)]
+    rs_b = [Scatter(lambda pos, h, j=j: pb[j].at[pos, :, c, :, part_of(h)], rb[j], t, y_of) for j in range(2)]
+
+    def send_others(j):
         one, two = rs_a[j], rs_b[j]
+        activate(one.far, j)
+        pair_a = down_a(one.far, j)
+
+        @pl.loop(1, RING)
+        def _(n):
+            activate(mod(one.far + n, RING), j)
+
+        pair_b = down_b(two.far, j)
         add_pair(pair_a, pa, qa, one.far, j)
         one.send_far()
         pair_a = down_a(one.right, j)
@@ -489,16 +503,8 @@
         pair_b = down_b(two.left, j)
         add_pair(pair_a, pa, qa, one.left, j)
         one.send_left()
-        pair_a = down_a(one.far, 1) if j == 0 else down_a(x, 0)
         add_pair(pair_b, pb, qb, two.left, j)
         two.send_left()
-        pair_b = down_b(two.far, 1) if j == 0 else down_b(t, 0)
-        if j == 0:
-            one.send_sums(adder(pa, j))
-            two.send_sums(adder(pb, j))
-    own_a, own_b = down_a(x, 1), down_b(t, 1)
-    add_pair(pair_a, pa, qa, x, 0)
-    add_pair(pair_b, pb, qb, t, 0)
 
     def finish_big(scatter, part, total, me, j):
         scatter.wait()
@@ -507,86 +513,100 @@
         def _(n):
             for h in range(2):
                 one, two = scatter.parts(h)
-                value = part[me, j, n, c, :, part_of(h)].astype(F32)
-                total[n, j, :, part_of(h)] = (value + one[n].astype(F32) + two[n].astype(F32)).astype(BF)
-
-    def small_a(j):
-        finish_big(rs_a[j], pa, ta, x, j)
-        small = Scatter(lambda pos, h: ta.at[pos, j, :, part_of(h)], sa.at[j], t, y_of)
-        small.send_far()
-        small.send_right()
-        small.send_left()
-        return small
-
-    def small_b(j):
-        finish_big(rs_b[j], pb, tb, t, j)
-        small = Scatter(lambda pos, h: tb.at[pos, j, :, part_of(h)], sb.at[j], x, x_of)
-        small.send_far()
-        small.send_right()
-        small.send_left()
-        return small
-
-    def small_adder(total, j):
-        def add(pos, h, slot):
-            own = total[pos, j, :, part_of(h)].astype(F32)
-            total[pos, j, :, part_of(h)] = (own + slot[...].astype(F32)).astype(BF)
-
-        return add
-
-    def finish_small(small, total, q, j):
-        small.wait()
-        for h in range(2):
-            one, two = small.parts(h)
-            value = total[small.me, j, :, part_of(h)].astype(F32)
-            res[q, :, part_of(h)] = (value + one[...].astype(F32) + two[...].astype(F32)).astype(BF)
-
-    take, take_extra = placing(True)
-
-    def take_out(q):
-        picked = dot(take, res[q]).astype(BF)
-        back_sent[:, :, spot(q) : spot(q) + lanes] = picked.reshape(experts, MAIN, lanes)
-
-    last_a, last_b = [small_a(0)], [small_b(0)]
+                value = part[j][me, n, c, :, part_of(h)].astype(F32)
+                total[j][n, :, part_of(h)] = (value + one[n].astype(F32) + two[n].astype(F32)).astype(BF)
+
+    def small_scatters(j):
+        smalls = []
+        for big, part, total, slots, me, to, of in (
+            (rs_a[j], pa, ta, sa, x, t, y_of),
+            (rs_b[j], pb, tb, sb, t, x, x_of),
+        ):
+            finish_big(big, part, total, me, j)
+            small = Scatter(lambda pos, h, total=total: total[j].at[pos, :, part_of(h)], slots[j], to, of)
+            small.send_far()
+            small.send_right()
+            small.send_left()
+            smalls.append(small)
+        return smalls
+
+    def small_sums(smalls, j):
+        for small, total in zip(smalls, (ta, tb)):
+
+            def add(pos, h, slot):
+                own = total[j][pos, :, part_of(h)].astype(F32)
+                total[j][pos, :, part_of(h)] = (own + slot[...].astype(F32)).astype(BF)
+
+            small.send_sums(add)
+
+    def send_back(smalls, j):
+        for small, total, result in zip(smalls, (ta, tb), (ea, eb)):
+            small.wait()
+            for h in range(2):
+                one, two = small.parts(h)
+                value = total[j][small.me, :, part_of(h)].astype(F32)
+                value = value + one[...].astype(F32) + two[...].astype(F32)
+                result[j][:, part_of(h)] = value.astype(BF)
+
+        def block(k):
+            at = k * 128 % lanes
+            return (ea if k * 128 < lanes else eb)[j][:, at : at + 128]
+
+        wide, take_extra = placing(j, True)
+        picked = sum(
+            dot(wide[b], jnp.concatenate([block(2 * p + b) for p in range(blocks // 2)], axis=1))
+            for b in range(2)
+        )
+        back_sent[:, :, starts[j] : starts[j] + lanes] = picked.astype(BF).reshape(experts, MAIN, lanes)
+        if j == 0:
+            extra = sum(dot(take_extra[k], block(k)) for k in range(blocks))
+            back_sent[:, :, extra_at : extra_at + 128] = extra.astype(BF).reshape(experts, MAIN, 128)
+        return exchange(back_sent, back, starts[j], ends[j])
+
+    def gated(j, k):
+        pieces = back[:, :, starts[j] + k // 2 * 128 : starts[j] + (k // 2 + 1) * 128].reshape(spread_rows, 128)
+        extras = back[:, :, extra_at : extra_at + 128].reshape(spread_rows, 128)
+        value = jnp.zeros((tokens, 128), F32)
+        for gate, n in ((1, 3), (2, 6)):
+            picked = dot(chosen_masks(n + 2 * j, float(k % 2))[:, :spread_rows], pieces)
+            if j == 0:
+                picked = picked + dot(chosen_masks(n + 1, 2.0 * k)[:, :spread_rows], extras)
+            value = value + keep[gate] * picked
+        return value
+
+    weights[2].wait()
+    send_others(0)
+    sides_1 = share_sides(big_1, 1)
+    own_a, own_b = down_a(x, 0), down_b(t, 0)
+    run(sides_1, 1)
+    far_1 = share_far(big_1, 1)
+    add_pair(own_a, pa, qa, x, 0)
+    add_pair(own_b, pb, qb, t, 0)
+    rs_a[0].send_sums(adder(pa, 0))
+    rs_b[0].send_sums(adder(pb, 0))
+    run(far_1, 1)
+    send_others(1)
+    own_a, own_b = down_a(x, 1), down_b(t, 1)
+    last_0 = small_scatters(0)
     add_pair(own_a, pa, qa, x, 1)
     add_pair(own_b, pb, qb, t, 1)
     rs_a[1].send_sums(adder(pa, 1))
     rs_b[1].send_sums(adder(pb, 1))
-    last_a[0].send_sums(small_adder(ta, 0))
-    last_b[0].send_sums(small_adder(tb, 0))
-    last_a.append(small_a(1))
-    last_b.append(small_b(1))
-    finish_small(last_a[0], ta, 0, 0)
-    finish_small(last_b[0], tb, 2, 0)
-    take_out(0)
-    take_out(2)
-    returning = [exchange(back_sent, back, 0, extra_at)]
-    last_a[1].send_sums(small_adder(ta, 1))
-    last_b[1].send_sums(small_adder(tb, 1))
-    finish_small(last_a[1], ta, 1, 1)
-    finish_small(last_b[1], tb, 3, 1)
-    take_out(1)
-    take_out(3)
-    extra = jnp.zeros((spread_rows, 128), F32)
-    for k in range(per_lane):
-        q, at = k * 128 // lanes, k * 128 % lanes
-        extra = extra + dot(take_extra[k], res[q, :, at : at + 128])
-    back_sent[:, :, extra_at : extra_at + 128] = extra.astype(BF).reshape(experts, MAIN, 128)
-    returning.append(exchange(back_sent, back, extra_at, share + 128))
+    small_sums(last_0, 0)
+    last_1 = small_scatters(1)
+    returning = [send_back(last_0, 0)]
+    small_sums(last_1, 1)
+    returning.append(send_back(last_1, 1))
     received(returning[0])
+    for k in range(blocks):
+        mixed[:, k * 128 : (k + 1) * 128] = gated(0, k)
     received(returning[1])
 
-    extras = back[:, :, extra_at : extra_at + 128].reshape(spread_rows, 128)
     cross = jnp.zeros((tokens, 1), F32)
     squares = jnp.zeros((tokens, 1), F32)
-    for k in range(share // 128):
-        at = spot(k * 128 // lanes) + k * 128 % lanes
-        block = back[:, :, at : at + 128].reshape(spread_rows, 128)
-        mixture = jnp.zeros((tokens, 128), F32)
-        for gate, n in ((1, 3), (2, 5)):
-            picked = dot(chosen_masks(n, 0.0)[:, :spread_rows], block)
-            picked = picked + dot(chosen_masks(n + 1, 2.0 * k)[:, :spread_rows], extras)
-            mixture = mixture + keep[gate] * picked
-        own = h_ref[:, pl.ds(pl.multiple_of(t * share + k * 128, 128), 128)].astype(F32)
+    for k in range(blocks):
+        mixture = mixed[:, k * 128 : (k + 1) * 128] + gated(1, k)
+        own = h_ref[:, own_lanes(k)].astype(F32)
         output = (own + mixture).astype(BF)
         out_ref[:, k * 128 : (k + 1) * 128] = output
         output = output.astype(F32)
@@ -626,12 +646,31 @@
     hidden = w_gate.shape[2]
     cap = max(2, 9 * tokens * top // (8 * experts))
     share = width // RING
-    lanes = share // RING
-    rows = experts * cap
+    lanes = share // 2
     piece = (experts, MAIN, share + 128)
     hbm = pl.BlockSpec(memory_space=pl.ANY)
     scratch = lambda shape, kind: pltpu.VMEM(shape, kind)
-    blocks = (RING, 2, RING, 2, rows, lanes)
+    rows = [experts * n for n in SLOTS]
+    assert sum(SLOTS) == cap
+    chunked = [
+        (lambda r: (RING, RING, 2, r, lanes), BF),
+        (lambda r: (RING, RING, 2, r, lanes), BF),
+        (lambda r: (RING, 2 * r, hidden), F32),
+        (lambda r: (RING, 2 * r, hidden), F32),
+        (lambda r: (RING, 2 * r, hidden), BF),
+        (lambda r: (RING, RING, 2, r, lanes), BF),
+        (lambda r: (RING, RING, 2, r, lanes), BF),
+        (lambda r: (RING, RING, r, lanes), BF),
+        (lambda r: (RING, RING, r, lanes), BF),
+        (lambda r: (6, RING, r, lanes // 2), BF),
+        (lambda r: (6, RING, r, lanes // 2), BF),
+        (lambda r: (RING, r, lanes), BF),
+        (lambda r: (RING, r, lanes), BF),
+        (lambda r: (6, r, lanes // 2), BF),
+        (lambda r: (6, r, lanes // 2), BF),
+        (lambda r: (r, lanes), BF),
+        (lambda r: (r, lanes), BF),
+    ]
     out, score = pl.pallas_call(
         functools.partial(kernel, (experts, cap)),
         out_shape=(
@@ -649,28 +688,16 @@
             scratch((hidden, width), BF),
             scratch((hidden, width), BF),
             scratch((hidden, width), BF),
+            scratch((width, hidden), BF),
+            scratch((width, hidden), BF),
             scratch((tokens, width), BF),
-            scratch((8, tokens, 128), F32),
+            scratch((9, tokens, 128), F32),
             scratch(piece, BF),
             scratch(piece, BF),
             scratch(piece, BF),
             scratch(piece, BF),
-            scratch(blocks, BF),
-            scratch(blocks, BF),
-            scratch((RING, 2 * rows, hidden), F32),
-            scratch((RING, 2 * rows, hidden), F32),
-            scratch((RING, 2 * rows, hidden), BF),
-            scratch(blocks, BF),
-            scratch(blocks, BF),
-            scratch((RING, 2, RING, rows, lanes), BF),
-            scratch((RING, 2, RING, rows, lanes), BF),
-            scratch((2, 6, RING, rows, lanes // 2), BF),
-            scratch((2, 6, RING, rows, lanes // 2), BF),
-            scratch((RING, 2, rows, lanes), BF),
-            scratch((RING, 2, rows, lanes), BF),
-            scratch((2, 6, rows, lanes // 2), BF),
-            scratch((2, 6, rows, lanes // 2), BF),
-            scratch((RING, rows, lanes), BF),
+            *[scratch(shape(r), kind) for shape, kind in chunked for r in rows],
+            scratch((tokens, share), F32),
             scratch((RING, tokens, 128), F32),
             scratch((experts, 8, 128), F32),
             scratch((2 * RING, 8, 128), F32),

time: 107 us -> 103 us (0.963)
  Pallas kernels: 103 us -> 98.7 us
    pallas_call x1, Pallas kernels: 103 us -> 98.7 us  [shards(): pl.pallas_call(functools.partial(kernel, (experts, cap)), out_shape=(jax....]
where the time goes in v3:
time: 103 us
  Pallas kernels  98.7 us (96%)
  between operations  2.45 us (2%)
  local copies, waits for them, and re-layouts  1.57 us (2%)
    pallas_call x1, Pallas kernels, shards(): pl.pallas_call(functools.partial(kernel, (experts, cap)), out_shape=(jax....  98.7 us

profile of v3, /device:TPU:1, one launch (start us, length us, event | category | flops | bytes accessed | tf_op | source)
XLA Modules:
  0.0 102.7 jit_solution(3711066782814438309)
XLA Ops:
  0.6 98.7 %layer.1 = (bf16[64,1024]{1,0:T(8,128)(2,1)}, f32[1,1]{1,0:T(1,128)}) custom-call(bf16[64,4096]{1,0:T(8,128)(2,1)} %bitcast.18, s32[2,64]{1,0:T(2,128)} %bitcast.22, f32[1,4096]{1,0:T(1,128)} %bitcast.21, bf16[8,4096]{1,0:T(8,128)(2,1)} %bitcast.20, bf16[448,4096]{1,0:T(8,128)(2,1)} %bitcast.15, bf16[448,4096]{1,0:T(8,128)(2,1)} %bitcast.16, ...), custom_call_target="tpu_custom_call" | custom-call | tf_op jit(solution)/shard_map/layer/pallas_call | solution.py:674
  99.4 1.6 %copy.11 = bf16[1,64,1024]{2,1,0:T(8,128)(2,1)} copy(bf16[1,64,1024]{2,1,0:T(8,128)(2,1)} %bitcast.19) | data formatting | bytes 262144

commit v4 on v3

--- a/solution.py
+++ b/solution.py
@@ -12,7 +12,7 @@
 BF = jnp.bfloat16
 F32 = jnp.float32
 RING = 4
-SENDS = 64
+SENDS = 40
 MAIN = 16
 SLOTS = (10, 8)
 WIDE = 8

time: 103 us -> 103 us (level)
  no operation moved by 1% of the time
where the time goes in v4:
time: 103 us
  Pallas kernels  98.5 us (96%)
  between operations  2.45 us (2%)
  local copies, waits for them, and re-layouts  1.57 us (2%)
    pallas_call x1, Pallas kernels, shards(): pl.pallas_call(functools.partial(kernel, (experts, cap)), out_shape=(jax....  98.5 us

profile of v4, /device:TPU:1, one launch (start us, length us, event | category | flops | bytes accessed | tf_op | source)
XLA Modules:
  0.0 102.5 jit_solution(3025047105490809579)
XLA Ops:
  0.6 98.5 %layer.1 = (bf16[64,1024]{1,0:T(8,128)(2,1)}, f32[1,1]{1,0:T(1,128)}) custom-call(bf16[64,4096]{1,0:T(8,128)(2,1)} %bitcast.18, s32[2,64]{1,0:T(2,128)} %bitcast.22, f32[1,4096]{1,0:T(1,128)} %bitcast.21, bf16[8,4096]{1,0:T(8,128)(2,1)} %bitcast.20, bf16[448,4096]{1,0:T(8,128)(2,1)} %bitcast.15, bf16[448,4096]{1,0:T(8,128)(2,1)} %bitcast.16, ...), custom_call_target="tpu_custom_call" | custom-call | tf_op jit(solution)/shard_map/layer/pallas_call | solution.py:674
  99.1 1.6 %copy.11 = bf16[1,64,1024]{2,1,0:T(8,128)(2,1)} copy(bf16[1,64,1024]{2,1,0:T(8,128)(2,1)} %bitcast.19) | data formatting | bytes 262144
